TPU v7x, 32 devices: a whole 2x2x4 slice. The times are simulated.
32 devices in a mesh: groups: 2 (over x), replica: 16 (over z, y, core).
Axes of the slice: x: 2, y: 2, z: 4, core: 2. Of those that a mesh axis runs over, the one named last changes fastest.
Arguments:
- tokens: bfloat16 [32768, 2048], P(('groups', 'replica')), parts along dimension 0, may hold values from -6 to 6
- pseudo_keys: bfloat16 [32, 2048, 512], P(('groups', 'replica')), parts along dimension 0, may hold values from -0.875 to 0.875
- pseudo_values: bfloat16 [32, 2048, 512], P(('groups', 'replica')), parts along dimension 0, may hold values from -0.875 to 0.875
- master_keys: float32 [4096, 512], P(('groups', 'replica')), parts along dimension 0, may hold values from -0.125 to 0.125
- moment_keys: float32 [4096, 512], P(('groups', 'replica')), parts along dimension 0, may hold values from -0.125 to 0.125
- master_values: float32 [4096, 512], P(('groups', 'replica')), parts along dimension 0, may hold values from -0.125 to 0.125
- moment_values: float32 [4096, 512], P(('groups', 'replica')), parts along dimension 0, may hold values from -0.125 to 0.125
- outer_hyper: float32 [4], P('groups'), parts along dimension 0, may hold values from 0.5 to 0.95
Outputs:
- eval_keys: bfloat16 [32768, 512], P(('groups', 'replica')), parts along dimension 0
- eval_values: bfloat16 [32768, 512], P(('groups', 'replica')), parts along dimension 0
- new_master_keys: float32 [4096, 512], P(('groups', 'replica')), parts along dimension 0
- new_moment_keys: float32 [4096, 512], P(('groups', 'replica')), parts along dimension 0
- new_master_values: float32 [4096, 512], P(('groups', 'replica')), parts along dimension 0
- new_moment_values: float32 [4096, 512], P(('groups', 'replica')), parts along dimension 0
There are 2 independent parts, one for each index of `groups`. A program takes and returns all parts, laid end to end along the dimension named above; each array names one. Nothing has to cross between parts.
All inputs are finite; a program needn't handle non-finite values.
Results may differ from a plain program's by a relative error of at most 0.0049.
Values may be sent and summed in bfloat16 or wider, within the bound.
A program may use at most 128 MiB of HBM per device.

v0:
```python
import functools

import jax
import jax.numpy as jnp
from jax import lax
from jax.experimental import pallas as pl
from jax.experimental.pallas import tpu as pltpu
from jax.sharding import PartitionSpec as P

MESH = pl.DeviceIdType.MESH
F32 = jnp.float32
BF16 = jnp.bfloat16


def kernel(
    Z,
    Y,
    replicas,
    tokens,
    pseudo_keys,
    pseudo_values,
    master_keys,
    moment_keys,
    master_values,
    moment_values,
    hyper,
    eval_keys,
    eval_values,
    out_master_keys,
    out_moment_keys,
    out_master_values,
    out_moment_values,
    tok,
    mine,
    from_core,
    to_y,
    from_y,
    to_z,
    from_left,
    from_right,
    weights,
    total,
    acc,
    result,
    master,
    moment,
    load_sem,
    state_sem,
    tok_sem,
    store_sem,
    rc_s,
    rc_r,
    ry_s,
    ry_r,
    rz_s,
    rl_r,
    rr_r,
    gr_s,
    gl_s,
    gz_r,
    gy_s,
    gy_r,
    gc_s,
    gc_r,
):
    me = lax.axis_index("replica")
    core = lax.rem(me, 2)
    chip = lax.div(me, 2)
    y = lax.rem(chip, Y)
    z = lax.div(chip, Y)
    oc = 1 - core
    oy = 1 - y

    def dev(zz, yy, cc):
        return {"replica": (zz * Y + yy) * 2 + cc}

    pseudo = (pseudo_keys, pseudo_values)
    rows = mine.shape[3]

    loads = [
        pltpu.make_async_copy(pseudo[kv].at[:, :, core], mine.at[kv], load_sem.at[kv])
        for kv in range(2)
    ]
    states = [
        pltpu.make_async_copy(src, dst, state_sem.at[i])
        for i, (src, dst) in enumerate(
            (
                (master_keys, master.at[0]),
                (moment_keys, moment.at[0]),
                (master_values, master.at[1]),
                (moment_values, moment.at[1]),
            )
        )
    ]
    blocks = tok.shape[0]
    depth = tok.shape[2]
    if len(tokens.shape) == 3:
        tok_loads = [
            pltpu.make_async_copy(tokens.at[q], tok.at[q], tok_sem.at[q]) for q in range(blocks)
        ]
    else:
        tok_loads = [
            pltpu.make_async_copy(
                tokens.at[:, q * depth : (q + 1) * depth], tok.at[q], tok_sem.at[q]
            )
            for q in range(blocks)
        ]

    def near(s):
        m = jnp.minimum(z, Z - 1 - z)
        half = lax.div(s + 1, 2)
        side = 2 * lax.rem(s + 1, 2) - 1
        beyond = jnp.where(z < Z - 1 - z, s, Z - 1 - s)
        return jnp.where(s <= 2 * m, z + half * side, beyond)

    def far(s):
        return near(Z - 1 - s)

    def steps(count, body, start=0):
        def run(s, carry):
            body(s)
            return carry

        lax.fori_loop(start, count, run, 0)

    def remote(src, dst, send, recv, device):
        return pltpu.make_async_remote_copy(
            src_ref=src,
            dst_ref=dst,
            send_sem=send,
            recv_sem=recv,
            device_id=device,
            device_id_type=MESH,
        )

    def core_copy(kv, p):
        return remote(
            pseudo[kv].at[p, :, oc],
            from_core.at[kv, p],
            rc_s.at[kv, p],
            rc_r.at[kv, p],
            dev(z, y, oc),
        )

    def y_copy(kv, p):
        return remote(
            to_y.at[kv, p], from_y.at[kv, p], ry_s.at[kv, p], ry_r.at[kv, p], dev(z, oy, core)
        )

    def right_copy(kv, p):
        return remote(
            to_z.at[kv, p], from_left.at[kv, p], rz_s.at[kv, p], rl_r.at[kv, p], dev(z + 1, y, core)
        )

    def left_copy(kv, p):
        return remote(
            to_z.at[kv, p], from_right.at[kv, p], rz_s.at[kv, p], rr_r.at[kv, p], dev(z - 1, y, core)
        )

    def w_right(kv, p):
        w = weights.at[kv, p, y, core]
        return remote(w, w, gr_s.at[kv, p], gz_r.at[kv, p], dev(z + 1, y, core))

    def w_left(kv, p):
        w = weights.at[kv, p, y, core]
        return remote(w, w, gl_s.at[kv, p], gz_r.at[kv, p], dev(z - 1, y, core))

    def w_y(kv, p, yy):
        w = weights.at[kv, p, yy, core]
        return remote(w, w, gy_s.at[kv, p], gy_r.at[kv, p], dev(z, oy, core))

    def w_core(kv, p, yy, cc):
        w = weights.at[kv, p, yy, cc]
        return remote(w, w, gc_s.at[kv, p, yy], gc_r.at[kv, p, yy], dev(z, y, oc))

    for copy in loads:
        copy.start()

    barrier = pltpu.get_barrier_semaphore()
    pl.semaphore_signal(barrier, inc=1, device_id=dev(z, y, oc), device_id_type=MESH)
    pl.semaphore_signal(barrier, inc=1, device_id=dev(z, oy, core), device_id_type=MESH)

    @pl.when(z > 0)
    def _():
        pl.semaphore_signal(barrier, inc=1, device_id=dev(z - 1, y, core), device_id_type=MESH)

    @pl.when(z < Z - 1)
    def _():
        pl.semaphore_signal(barrier, inc=1, device_id=dev(z + 1, y, core), device_id_type=MESH)

    peers = 2 + jnp.where(z > 0, 1, 0) + jnp.where(z < Z - 1, 1, 0)
    pl.semaphore_wait(barrier, peers)

    for kv in range(2):
        steps(Z, lambda s: core_copy(kv, far(s)).start())
    for copy in states + tok_loads:
        copy.start()

    for kv in range(2):
        loads[kv].wait()

        def y_send(s):
            p = far(s)
            core_copy(kv, p).wait_recv()
            both = mine[kv, p, oy].astype(F32) + from_core[kv, p, oy].astype(F32)
            to_y[kv, p] = both.astype(BF16)
            y_copy(kv, p).start()

        steps(Z, y_send)

    acc[...] = jnp.zeros_like(acc)

    def reduce_step(kv, s):
        p = far(s)
        y_copy(kv, p).wait_recv()
        total[...] = (
            mine[kv, p, y].astype(F32)
            + from_core[kv, p, y].astype(F32)
            + from_y[kv, p].astype(F32)
        )

        @pl.when((p >= z) & (z > 0))
        def _():
            right_copy(kv, p).wait_recv()
            total[...] += from_left[kv, p].astype(F32)

        @pl.when((p <= z) & (z < Z - 1))
        def _():
            left_copy(kv, p).wait_recv()
            total[...] += from_right[kv, p].astype(F32)

        @pl.when(p != z)
        def _():
            to_z[kv, p] = total[...].astype(BF16)

        @pl.when(p > z)
        def _():
            right_copy(kv, p).start()

        @pl.when(p < z)
        def _():
            left_copy(kv, p).start()

    def nesterov(kv):
        outer_rate = hyper[0]
        outer_mom = hyper[1]
        averaged = total[...] / replicas
        moment_new = outer_mom * moment[kv] + averaged
        master_new = master[kv] - outer_rate * (averaged + outer_mom * moment_new)
        weights[kv, z, y, core] = master_new.astype(BF16)
        master[kv] = master_new
        moment[kv] = moment_new

    def spread(kv, p):
        @pl.when((p <= z) & (z < Z - 1))
        def _():
            w_right(kv, p).start()

        @pl.when((p >= z) & (z > 0))
        def _():
            w_left(kv, p).start()

        w_y(kv, p, y).start()
        w_core(kv, p, y, core).start()

    def gather_step(kv, s):
        p = near(s)
        w_right(kv, p).wait_recv()
        spread(kv, p)

    tile = min(1024, acc.shape[1])
    cols = 256
    across = acc.shape[2] // cols

    def dot(kv, p):
        for yy in range(Y):
            w_core(kv, p, yy, oc).wait_recv()

        def one(i, carry):
            m, n = lax.div(i, across), lax.rem(i, across)
            span = pl.ds(pl.multiple_of(m * tile, tile), tile)
            lane = pl.ds(pl.multiple_of(n * cols, cols), cols)
            part = acc[kv, span, lane]
            for yy in range(Y):
                block = weights[kv, p, yy, :, :, lane].reshape(2 * rows, cols)
                part += jnp.dot(tok[p * Y + yy, span, :], block, preferred_element_type=F32)
            acc[kv, span, lane] = part
            return carry

        lax.fori_loop(0, acc.shape[1] // tile * across, one, 0)

    def y_arrival(kv, s):
        p = near(s)
        w_y(kv, p, oy).wait_recv()
        w_core(kv, p, oy, core).start()

    outs = ((out_master_keys, out_moment_keys), (out_master_values, out_moment_values))

    def stores(kv):
        return [
            pltpu.make_async_copy(master.at[kv], outs[kv][0], store_sem.at[2 * kv]),
            pltpu.make_async_copy(moment.at[kv], outs[kv][1], store_sem.at[2 * kv + 1]),
        ]

    evals = [
        pltpu.make_async_copy(result.at[kv], out, store_sem.at[4 + kv])
        for kv, out in enumerate((eval_keys, eval_values))
    ]

    steps(Z, lambda s: reduce_step(0, s))
    states[0].wait()
    states[1].wait()
    nesterov(0)
    spread(0, z)
    for copy in stores(0):
        copy.start()

    reduce_step(1, 0)

    def reduce_and_gather(s):
        reduce_step(1, s)
        gather_step(0, s)

    steps(Z - 1, reduce_and_gather, 1)
    reduce_step(1, Z - 1)
    states[2].wait()
    states[3].wait()
    nesterov(1)
    spread(1, z)
    for copy in stores(1):
        copy.start()
    gather_step(0, Z - 1)
    for copy in tok_loads:
        copy.wait()

    def second(s):
        gather_step(1, s + 1)
        y_arrival(0, s)

    steps(Z - 1, second)
    y_arrival(0, Z - 1)
    steps(Z, lambda s: dot(0, near(s)))
    result[0] = acc[0].astype(BF16)
    evals[0].start()

    def last(s):
        y_arrival(1, s)
        dot(1, near(s))

    steps(Z, last)
    result[1] = acc[1].astype(BF16)
    evals[1].start()

    for kv in range(2):

        def drain(p):
            core_copy(kv, p).wait_send()
            y_copy(kv, p).wait_send()

            @pl.when(p != z)
            def _():
                right_copy(kv, p).wait_send()

            @pl.when((p <= z) & (z < Z - 1))
            def _():
                w_right(kv, p).wait_send()

            @pl.when((p >= z) & (z > 0))
            def _():
                w_left(kv, p).wait_send()

            w_y(kv, p, y).wait_send()
            w_core(kv, p, y, core).wait_send()
            w_core(kv, p, oy, core).wait_send()

        steps(Z, drain)
        for copy in stores(kv):
            copy.wait()
    for copy in evals:
        copy.wait()


def place(*refs):
    source, target, held = refs[:6], refs[6:12], refs[12:18]
    in_sem, out_sem = refs[18:]
    order = (2, 3, 4, 5, 0, 1)
    loads = {i: pltpu.make_async_copy(source[i], held[i], in_sem.at[i]) for i in order}
    stores = {i: pltpu.make_async_copy(held[i], target[i], out_sem.at[i]) for i in order}
    for i in order:
        loads[i].start()
    for i in order:
        loads[i].wait()
        stores[i].start()
    for i in order:
        stores[i].wait()


def body(
    tokens,
    pseudo_keys,
    pseudo_values,
    master_keys,
    moment_keys,
    master_values,
    moment_values,
    outer_hyper,
):
    replicas = lax.axis_size("replica")
    Y = 2
    Z = replicas // (2 * Y)
    width = master_keys.shape[1]
    rows = master_keys.shape[0]
    count = tokens.shape[0]
    blocks = Z * Y
    depth = 2 * rows
    if depth % 128:
        tokens = tokens.reshape(count, blocks, depth).swapaxes(0, 1)
    pseudo_keys, pseudo_values = (
        p.reshape(Z, Y, 2, rows, width) for p in (pseudo_keys, pseudo_values)
    )
    hbm = pl.BlockSpec(memory_space=pl.ANY)
    dma = pltpu.SemaphoreType.DMA
    state = jax.ShapeDtypeStruct(master_keys.shape, F32)
    evaluated = jax.ShapeDtypeStruct((count, width), BF16)
    part = pltpu.VMEM((2, Z, rows, width), BF16)
    pair = pltpu.VMEM((2, Z, Y, rows, width), BF16)
    unit = dma((2, Z))
    results = pl.pallas_call(
        functools.partial(kernel, Z, Y, replicas),
        out_shape=(evaluated, evaluated, state, state, state, state),
        in_specs=[hbm] * 7 + [pl.BlockSpec(memory_space=pltpu.SMEM)],
        out_specs=(hbm,) * 6,
        scratch_shapes=[
            pltpu.VMEM((blocks, count, depth), BF16),
            pair,
            pair,
            part,
            part,
            part,
            part,
            part,
            pltpu.VMEM((2, Z, Y, 2, rows, width), BF16),
            pltpu.VMEM((rows, width), F32),
            pltpu.VMEM((2, count, width), F32),
            pltpu.VMEM((2, count, width), BF16),
            pltpu.VMEM((2, rows, width), F32),
            pltpu.VMEM((2, rows, width), F32),
            dma((2,)),
            dma((4,)),
            dma((blocks,)),
            dma((6,)),
            unit,
            unit,
            unit,
            unit,
            unit,
            unit,
            unit,
            unit,
            unit,
            unit,
            unit,
            unit,
            dma((2, Z, Y)),
            dma((2, Z, Y)),
        ],
        compiler_params=pltpu.CompilerParams(
            collective_id=0, has_side_effects=True, vmem_limit_bytes=60 * 1024 * 1024
        ),
        name="outer_step",
    )(
        tokens,
        pseudo_keys,
        pseudo_values,
        master_keys,
        moment_keys,
        master_values,
        moment_values,
        outer_hyper,
    )
    return pl.pallas_call(
        place,
        out_shape=tuple(jax.ShapeDtypeStruct(a.shape, a.dtype) for a in results),
        in_specs=[hbm] * 6,
        out_specs=(hbm,) * 6,
        scratch_shapes=[pltpu.VMEM(a.shape, a.dtype) for a in results] + [dma((6,)), dma((6,))],
        name="place",
    )(*results)


def solution(mesh):
    rows = P(("groups", "replica"), None)
    stack = P(("groups", "replica"), None, None)
    return jax.shard_map(
        body,
        mesh=mesh,
        in_specs=(rows, stack, stack, rows, rows, rows, rows, P("groups")),
        out_specs=(rows,) * 6,
        check_vma=False,
    )
```

profile of v0, /device:TPU:0, one launch (start us, length us, event | category | flops | bytes accessed | tf_op | source)
XLA Modules:
  0.0 73.7 jit_solution(13948613527990069502)
XLA Ops:
  0.6 70.1 %outer_step.1 = (bf16[1024,512]{1,0:T(8,128)(2,1)}, bf16[1024,512]{1,0:T(8,128)(2,1)}, f32[128,512]{1,0:T(8,128)}, f32[128,512]{1,0:T(8,128)}, f32[128,512]{1,0:T(8,128)}, /*index=5*/f32[128,512]{1,0:T(8,128)}) custom-call(bf16[1024,2048]{1,0:T(8,128)(2,1)} %tokens.1, bf16[4,2,2,128,512]{4,3,2,1,0:T(8,128)(2,1)} %bitcast.2, ...), custom_call_target="tpu_custom_call" | custom-call | tf_op jit(solution)/shard_map/outer_step/pallas_call | solution.py:428
  70.8 3.0 %place.1 = (bf16[1024,512]{1,0:T(8,128)(2,1)}, bf16[1024,512]{1,0:T(8,128)(2,1)}, f32[128,512]{1,0:T(8,128)}, f32[128,512]{1,0:T(8,128)}, f32[128,512]{1,0:T(8,128)}, /*index=5*/f32[128,512]{1,0:T(8,128)}) custom-call(bf16[1024,512]{1,0:T(8,128)(2,1)} %get-tuple-element.12.refs_0_, bf16[1024,512]{1,0:T(8,128)(2,1)} %get-tuple-element.13.refs_1_, ...), custom_call_target="tpu_custom_call" | custom-call | tf_op jit(solution)/shard_map/place/pallas_call | solution.py:481
where the time goes:
time: 73.9 us; the launch traced here: 73.7 us
  Pallas kernels  73.1 us (99%)
    pallas_call x1, Pallas kernels, body(): pl.pallas_call(functools.partial(kernel, Z, Y, replicas), out_shape=(eval...  70.1 us
    pallas_call x1, Pallas kernels, body(): pl.pallas_call(place, out_shape=tuple((jax.ShapeDtypeStruct(a.shape, a.dt...  2.97 us

commit v1 on v0

v1 whole, which is shorter than its diff:
```python
import functools

import jax
import jax.numpy as jnp
from jax import lax
from jax.experimental import pallas as pl
from jax.experimental.pallas import tpu as pltpu
from jax.sharding import PartitionSpec as P

MESH = pl.DeviceIdType.MESH
F32 = jnp.float32
BF16 = jnp.bfloat16

REDUCE = "ABAA"
GATHER = "AAAB"

TUNED = (
    ("Y", 0, 0), ("Y", 0, 1), ("Y", 0, 3), ("Z", 1, 0), ("Y", 2, 0), ("Y", 3, 0), ("Y", 2, 1), ("Y", 2, 2),
    ("Y", 3, 3), ("Y", 0, 2), ("Y", 2, 3), ("Y", 3, 1), ("Z", 0, 0), ("Z", 1, 1), ("Z", 1, 2), ("Z", 2, 0),
    ("Z", 3, 0), ("Z", 0, 1), ("Z", 0, 2), ("Z", 1, 3), ("Y", 3, 2), ("Z", 2, 1), ("Z", 3, 1), ("Z", 2, 2),
    ("Z", 0, 3), ("F", 0, 0), ("F", 1, 0), ("Z", 2, 3), ("F", 2, 0), ("Z", 3, 2), ("G", 0, 1), ("G", 1, 1),
    ("H", 2, 0), ("H", 0, 0), ("G", 2, 1), ("G", 1, 2), ("Z", 3, 3), ("F", 3, 0), ("D", 0, 0), ("D", 2, 0),
    ("H", 1, 0), ("G", 1, 3), ("G", 0, 2), ("H", 1, 1), ("D", 1, 0), ("G", 3, 1), ("H", 0, 1), ("G", 2, 2),
    ("H", 3, 0), ("H", 2, 1), ("G", 3, 2), ("D", 1, 1), ("D", 3, 0), ("G", 0, 3), ("D", 2, 1), ("H", 1, 3),
    ("H", 1, 2), ("D", 0, 1), ("G", 2, 3), ("H", 0, 2), ("K", 3, 1), ("D", 1, 2), ("D", 1, 3), ("H", 2, 2),
    ("K", 3, 2), ("D", 3, 1), ("G", 3, 3), ("H", 0, 3), ("D", 0, 2), ("D", 2, 2), ("H", 2, 3), ("D", 0, 3),
    ("K", 3, 3), ("D", 3, 2), ("D", 2, 3), ("D", 3, 3),
)


def plan(Z):
    steps = 1 + max(s for _, _, s in TUNED)
    if steps == Z:
        return TUNED
    units = range(len(REDUCE))
    order = [("Y", u, None) for u in units if REDUCE[u] == "A"]
    for u in units:
        order += [("Z", u, None), ("Z", u, Z - 1), ("F", u, 0)]
    for u in units:
        order += [("G", u, None)]
        order += [("H", u, None)] if GATHER[u] == "A" else [("H", u, 0), ("K", u, None)]
        order += [("D", u, 0), ("D", u, None), ("D", u, Z - 1)]
    return order


def kernel(
    Z,
    Y,
    replicas,
    tokens,
    pseudo_keys,
    pseudo_values,
    master_keys,
    moment_keys,
    master_values,
    moment_values,
    hyper_in,
    eval_keys,
    eval_values,
    out_master_keys,
    out_moment_keys,
    out_master_values,
    out_moment_values,
    tok,
    mine,
    from_core,
    to_y,
    from_y,
    to_z,
    from_left,
    from_right,
    weights,
    total,
    acc,
    master,
    moment,
    hyper,
    load_sem,
    state_sem,
    tok_sem,
    rc_s,
    rc_r,
    ry_s,
    ry_r,
    rz_s,
    rl_r,
    rr_r,
    gr_s,
    gl_s,
    gz_r,
    gy_s,
    gy_r,
    gc_s,
    gc_r,
):
    me = lax.axis_index("replica")
    core = lax.rem(me, 2)
    chip = lax.div(me, 2)
    y = lax.rem(chip, Y)
    z = lax.div(chip, Y)
    oc = 1 - core
    oy = 1 - y

    def dev(zz, yy, cc):
        return {"replica": (zz * Y + yy) * 2 + cc}

    pseudo = (pseudo_keys, pseudo_values)
    evals = (eval_keys, eval_values)
    states = ((out_master_keys, out_moment_keys), (out_master_values, out_moment_values))
    units = mine.shape[0]
    halves = units // 2
    rows, cols = mine.shape[3:]
    count = tok.shape[1]
    depth = tok.shape[2]

    def kv_of(u):
        return u // halves

    def lanes(u):
        return pl.ds((u % halves) * cols, cols)

    loads = [
        pltpu.make_async_copy(
            pseudo[kv_of(u)].at[:, :, core, :, lanes(u)], mine.at[u], load_sem.at[u]
        )
        for u in range(units)
    ]
    state_loads = [
        pltpu.make_async_copy(src, dst, state_sem.at[i])
        for i, (src, dst) in enumerate(
            (
                (master_keys, master.at[0]),
                (moment_keys, moment.at[0]),
                (master_values, master.at[1]),
                (moment_values, moment.at[1]),
                (hyper_in, hyper),
            )
        )
    ]
    if len(tokens.shape) == 3:
        tok_loads = [
            pltpu.make_async_copy(tokens.at[p], tok.at[p], tok_sem.at[p]) for p in range(Z)
        ]
    else:
        tok_loads = [
            pltpu.make_async_copy(
                tokens.at[:, p * depth : (p + 1) * depth], tok.at[p], tok_sem.at[p]
            )
            for p in range(Z)
        ]

    upper = 2 * z >= Z
    m = jnp.minimum(z, Z - 1 - z)

    def near(s):
        half = (s + 1) // 2 if isinstance(s, int) else lax.div(s + 1, 2)
        side = 2 * (s % 2) - 1 if isinstance(s, int) else 2 * lax.rem(s, 2) - 1
        place = jnp.where(s <= 2 * m, m + half * side, s)
        return jnp.where(upper, Z - 1 - place, place)

    def far(s):
        return near(Z - 1 - s)

    def remote(src, dst, send, recv, device):
        return pltpu.make_async_remote_copy(
            src_ref=src,
            dst_ref=dst,
            send_sem=send,
            recv_sem=recv,
            device_id=device,
            device_id_type=MESH,
        )

    def core_copy(u, p):
        return remote(
            pseudo[kv_of(u)].at[p, :, oc, :, lanes(u)],
            from_core.at[u, p],
            rc_s.at[u, p],
            rc_r.at[u, p],
            dev(z, y, oc),
        )

    def y_copy(u, p):
        return remote(
            to_y.at[u, p], from_y.at[u, p], ry_s.at[u, p], ry_r.at[u, p], dev(z, oy, core)
        )

    def z_refs(u, p):
        if REDUCE[u] == "A":
            return to_z.at[u, p, 0], from_left.at[u, p, 0], from_right.at[u, p, 0]
        return to_z.at[u, p], from_left.at[u, p], from_right.at[u, p]

    def right_copy(u, p):
        src, dst, _ = z_refs(u, p)
        return remote(src, dst, rz_s.at[u, p], rl_r.at[u, p], dev(z + 1, y, core))

    def left_copy(u, p):
        src, _, dst = z_refs(u, p)
        return remote(src, dst, rz_s.at[u, p], rr_r.at[u, p], dev(z - 1, y, core))

    def w_right(u, p, yy):
        w = weights.at[u, p, yy, core]
        return remote(w, w, gr_s.at[u, p, yy], gz_r.at[u, p, yy], dev(z + 1, y, core))

    def w_left(u, p, yy):
        w = weights.at[u, p, yy, core]
        return remote(w, w, gl_s.at[u, p, yy], gz_r.at[u, p, yy], dev(z - 1, y, core))

    def w_y(u, p, yy):
        w = weights.at[u, p, yy, core]
        return remote(w, w, gy_s.at[u, p], gy_r.at[u, p], dev(z, oy, core))

    def w_core(u, p, yy, cc):
        w = weights.at[u, p, yy, cc]
        return remote(w, w, gc_s.at[u, p, yy], gc_r.at[u, p, yy], dev(z, y, oc))

    for copy in loads:
        copy.start()

    barrier = pltpu.get_barrier_semaphore()
    pl.semaphore_signal(barrier, inc=1, device_id=dev(z, y, oc), device_id_type=MESH)
    pl.semaphore_signal(barrier, inc=1, device_id=dev(z, oy, core), device_id_type=MESH)

    @pl.when(z > 0)
    def _():
        pl.semaphore_signal(barrier, inc=1, device_id=dev(z - 1, y, core), device_id_type=MESH)

    @pl.when(z < Z - 1)
    def _():
        pl.semaphore_signal(barrier, inc=1, device_id=dev(z + 1, y, core), device_id_type=MESH)

    peers = 2 + jnp.where(z > 0, 1, 0) + jnp.where(z < Z - 1, 1, 0)
    pl.semaphore_wait(barrier, peers)

    def each(first, last, body):
        def run(s, carry):
            body(s)
            return carry

        lax.fori_loop(first, last, run, 0)

    for u in range(units):
        each(0, Z, lambda s: core_copy(u, far(s)).start())
    for copy in state_loads + tok_loads:
        copy.start()

    loaded = set()

    def once(name, copy):
        if name not in loaded:
            loaded.add(name)
            copy.wait()

    def pair_sum(u, p, *yy):
        index = (u, p) + yy
        return mine[index].astype(F32) + from_core[index].astype(F32)

    def reduce_y(u, s):
        p = far(s)
        core_copy(u, p).wait_recv()
        to_y[u, p] = pair_sum(u, p, oy).astype(BF16)
        y_copy(u, p).start()

    def reduce_z(u, s, last):
        p = far(s)
        first = REDUCE[u] == "A"
        if first:
            y_copy(u, p).wait_recv()
            part = total.at[u, y]
            part[...] = pair_sum(u, p, y) + from_y[u, p].astype(F32)
        else:
            core_copy(u, p).wait_recv()
            part = total.at[u]
            part[...] = pair_sum(u, p)
        out, left, right = z_refs(u, p)

        @pl.when((p >= z) & (z > 0))
        def _():
            right_copy(u, p).wait_recv()
            part[...] += left[...].astype(F32)

        @pl.when((p <= z) & (z < Z - 1))
        def _():
            left_copy(u, p).wait_recv()
            part[...] += right[...].astype(F32)

        if not last:
            out[...] = part[...].astype(BF16)

            @pl.when(p > z)
            def _():
                right_copy(u, p).start()

            @pl.when(p < z)
            def _():
                left_copy(u, p).start()
        elif not first:
            to_y[u, z] = total[u, oy].astype(BF16)
            y_copy(u, z).start()

    def spread(u, p, yy):
        @pl.when((p <= z) & (z < Z - 1))
        def _():
            w_right(u, p, yy).start()

        @pl.when((p >= z) & (z > 0))
        def _():
            w_left(u, p, yy).start()

    def update(u):
        kv, lane = kv_of(u), lanes(u)
        summed = total[u, y]
        if REDUCE[u] == "B":
            y_copy(u, z).wait_recv()
            summed += from_y[u, z].astype(F32)
        for i in (4, 2 * kv, 2 * kv + 1):
            once(("state", i), state_loads[i])
        outer_rate = hyper[0]
        outer_mom = hyper[1]
        averaged = summed / replicas
        moment_new = outer_mom * moment[kv, :, lane] + averaged
        master_new = master[kv, :, lane] - outer_rate * (averaged + outer_mom * moment_new)
        weights[u, z, y, core] = master_new.astype(BF16)
        if GATHER[u] == "A":
            spread(u, z, y)
            w_y(u, z, y).start()
        else:
            w_y(u, z, y).start()
            spread(u, z, y)
        w_core(u, z, y, core).start()
        master_out, moment_out = states[kv]
        master_out[:, lane] = master_new
        moment_out[:, lane] = moment_new

    def pass_z(u, s, yy):
        p = near(s)
        w_right(u, p, yy).wait_recv()
        spread(u, p, yy)
        if GATHER[u] == "A":
            w_y(u, p, yy).start()
        w_core(u, p, yy, core).start()

    def pass_y(u, s):
        p = near(s)
        w_y(u, p, oy).wait_recv()
        if GATHER[u] == "B":
            spread(u, p, oy)
        w_core(u, p, oy, core).start()

    tile = min(1024, count)

    def dot(u, s, place):
        p = near(s)
        for yy in range(Y):
            w_core(u, p, yy, oc).wait_recv()
        block = weights[u, p].reshape(2 * Y * rows, cols)

        def one(i):
            span = pl.ds(i * tile if isinstance(i, int) else pl.multiple_of(i * tile, tile), tile)
            part = jnp.dot(tok[p, span, :], block, preferred_element_type=F32)
            if place != "first":
                part += acc[u, span, :]
            if place == "last":
                evals[kv_of(u)][span, lanes(u)] = part.astype(BF16)
            else:
                acc[u, span, :] = part

        if count == tile:
            one(0)
        else:
            each(0, count // tile, one)

    def take(kind, u, s):
        if kind == "Y":
            once(("load", u), loads[u])
            if s is None:
                each(0, Z, lambda t: reduce_y(u, t))
            else:
                reduce_y(u, s)
        elif kind == "Z":
            once(("load", u), loads[u])
            if s is None:
                each(0, Z - 1, lambda t: reduce_z(u, t, False))
            else:
                reduce_z(u, s, s == Z - 1)
        elif kind == "F":
            update(u)
        elif kind in ("G", "K"):
            yy = y if kind == "G" else oy
            if s is None:
                each(1, Z, lambda t: pass_z(u, t, yy))
            else:
                pass_z(u, s, yy)
        elif kind == "H":
            if s is None:
                each(0, Z, lambda t: pass_y(u, t))
            else:
                pass_y(u, s)
        else:
            for i, copy in enumerate(tok_loads):
                once(("tokens", i), copy)
            if s is None:
                each(1, Z - 1, lambda t: dot(u, t, "middle"))
            else:
                dot(u, s, "first" if s == 0 else "last" if s == Z - 1 else "middle")

    for kind, u, s in plan(Z):
        take(kind, u, s)

    def sent(u, p, yy):
        @pl.when((p <= z) & (z < Z - 1))
        def _():
            w_right(u, p, yy).wait_send()

        @pl.when((p >= z) & (z > 0))
        def _():
            w_left(u, p, yy).wait_send()

    for u in range(units):

        def drain(p):
            core_copy(u, p).wait_send()
            if REDUCE[u] == "A":
                y_copy(u, p).wait_send()

            @pl.when(p != z)
            def _():
                right_copy(u, p).wait_send()

            sent(u, p, y)
            if GATHER[u] == "A":
                w_y(u, p, y).wait_send()
            else:
                sent(u, p, oy)
            w_core(u, p, y, core).wait_send()
            w_core(u, p, oy, core).wait_send()

        each(0, Z, drain)
        if REDUCE[u] == "B":
            y_copy(u, z).wait_send()
        if GATHER[u] == "B":
            w_y(u, z, y).wait_send()


def place(*refs):
    source, target, sem = refs[:6], refs[6:12], refs[12]
    stores = [pltpu.make_async_copy(source[i], target[i], sem.at[i]) for i in range(6)]
    for copy in stores:
        copy.start()
    for copy in stores:
        copy.wait()


def body(
    tokens,
    pseudo_keys,
    pseudo_values,
    master_keys,
    moment_keys,
    master_values,
    moment_values,
    outer_hyper,
):
    replicas = lax.axis_size("replica")
    Y = 2
    Z = replicas // (2 * Y)
    width = master_keys.shape[1]
    rows = master_keys.shape[0]
    count = tokens.shape[0]
    units = len(REDUCE)
    cols = 2 * width // units
    depth = 2 * Y * rows
    if depth % 128:
        tokens = tokens.reshape(count, Z, depth).swapaxes(0, 1)
    pseudo_keys, pseudo_values = (
        p.reshape(Z, Y, 2, rows, width) for p in (pseudo_keys, pseudo_values)
    )
    hbm = pl.BlockSpec(memory_space=pltpu.HBM)
    vmem = pl.BlockSpec(memory_space=pltpu.VMEM)
    dma = pltpu.SemaphoreType.DMA
    state = (master_keys.shape, F32)
    evaluated = ((count, width), BF16)
    shapes = (evaluated, evaluated, state, state, state, state)
    single = pltpu.VMEM((units, Z, rows, cols), BF16)
    double = pltpu.VMEM((units, Z, Y, rows, cols), BF16)
    results = pl.pallas_call(
        functools.partial(kernel, Z, Y, replicas),
        out_shape=tuple(pltpu.VMEM(*a) for a in shapes),
        in_specs=[hbm] * 8,
        out_specs=(vmem,) * 6,
        scratch_shapes=[
            pltpu.VMEM((Z, count, depth), BF16),
            double,
            double,
            single,
            single,
            double,
            double,
            double,
            pltpu.VMEM((units, Z, Y, 2, rows, cols), BF16),
            pltpu.VMEM((units, Y, rows, cols), F32),
            pltpu.VMEM((units, count, cols), F32),
            pltpu.VMEM((2, rows, width), F32),
            pltpu.VMEM((2, rows, width), F32),
            pltpu.SMEM((2,), F32),
            dma((units,)),
            dma((5,)),
            dma((Z,)),
            *[dma((units, Z))] * 7,
            *[dma((units, Z, Y))] * 3,
            *[dma((units, Z))] * 2,
            *[dma((units, Z, Y))] * 2,
        ],
        compiler_params=pltpu.CompilerParams(
            collective_id=0, has_side_effects=True, vmem_limit_bytes=50 * 1024 * 1024
        ),
        name="outer_step",
    )(
        *[
            pltpu.with_memory_space_constraint(a, pltpu.HBM)
            for a in (
                tokens,
                pseudo_keys,
                pseudo_values,
                master_keys,
                moment_keys,
                master_values,
                moment_values,
                outer_hyper,
            )
        ]
    )
    return pl.pallas_call(
        place,
        out_shape=tuple(jax.ShapeDtypeStruct(*a) for a in shapes),
        in_specs=[vmem] * 6,
        out_specs=(hbm,) * 6,
        scratch_shapes=[dma((6,))],
        name="place",
    )(*[pltpu.with_memory_space_constraint(r, pltpu.VMEM) for r in results])


def solution(mesh):
    rows = P(("groups", "replica"), None)
    stack = P(("groups", "replica"), None, None)
    return jax.shard_map(
        body,
        mesh=mesh,
        in_specs=(rows, stack, stack, rows, rows, rows, rows, P("groups")),
        out_specs=(rows,) * 6,
        check_vma=False,
    )
```

time: 73.9 us -> 59.9 us (0.81)
  Pallas kernels: 73.1 us -> 59.2 us
    pallas_call x2, Pallas kernels: 73.1 us -> 59.2 us  [the longest x1 57.5 us: body(): pl.pallas_call(functools.partial(kernel, Z, Y, replicas), out_shape=tuple...]
where the time goes in v1:
time: 59.9 us; the launch traced here: 59.8 us
  Pallas kernels  59.2 us (99%)
  between operations  0.64 us (1%)
    pallas_call x1, Pallas kernels, body(): pl.pallas_call(functools.partial(kernel, Z, Y, replicas), out_shape=tuple...  57.5 us
    pallas_call x1, Pallas kernels, body(): pl.pallas_call(place, out_shape=tuple((jax.ShapeDtypeStruct(*a) for a in...  1.71 us

profile of v1, /device:TPU:0, one launch (start us, length us, event | category | flops | bytes accessed | tf_op | source)
XLA Modules:
  0.0 59.8 jit_solution(10911170010427802810)
XLA Ops:
  0.6 57.5 %outer_step.1 = (bf16[1024,512]{1,0:T(8,128)(2,1)S(1)}, bf16[1024,512]{1,0:T(8,128)(2,1)S(1)}, f32[128,512]{1,0:T(8,128)S(1)}, f32[128,512]{1,0:T(8,128)S(1)}, f...) custom-call(bf16[1024,2048]{1,0:T(8,128)(2,1)} %tokens.1, bf16[4,2,2,128,512]{4,3,2,1,0:T(8,128)(2,1)} %bitcast.2, ...), custom_call_target="tpu_custom_call" | custom-call | tf_op jit(solution)/shard_map/outer_step/pallas_call | solution.py:486
  58.1 1.7 %place.1 = (bf16[1024,512]{1,0:T(8,128)(2,1)}, bf16[1024,512]{1,0:T(8,128)(2,1)}, f32[128,512]{1,0:T(8,128)}, f32[128,512]{1,0:T(8,128)}, f32[128,512]{1,0:T(8,128)}, /*index=5*/f32[128,512]{1,0:T(8,128)}) custom-call(bf16[1024,512]{1,0:T(8,128)(2,1)S(1)} %get-tuple-element.12.refs_0_, bf16[1024,512]{1,0:T(8,128)(2,1)S(1)} %get-tuple-element.13.refs_1_, ...), custom_call_target="tpu_custom_call" | custom-call | tf_op jit(solution)/shard_map/place/pallas_call | solution.py:533

commit v2 on v1

v2 whole, which is shorter than its diff:
```python
import functools

import jax
import jax.numpy as jnp
from jax import lax
from jax.experimental import pallas as pl
from jax.experimental.pallas import tpu as pltpu
from jax.sharding import PartitionSpec as P

MESH = pl.DeviceIdType.MESH
F32 = jnp.float32
BF16 = jnp.bfloat16

UNITS = ((0, 0), (0, 1), (1, 0), (1, 1))
PARTS = (
    (0, 0, 6, "A", "A"),
    (0, 6, 8, "B", "A"),
    (1, 0, 6, "A", "A"),
    (1, 6, 8, "B", "B"),
    (2, 0, 6, "A", "A"),
    (2, 6, 8, "B", "B"),
    (3, 0, 6, "A", "A"),
    (3, 6, 8, "A", "B"),
)

BATCHES = ((0, 2, 0, 2), (0, 2, 2, 4), (2, 4, 0, 1), (2, 4, 1, 2), (2, 4, 2, 4))
TUNED = (
    ("C", 0, 0), ("Y", 0, 0), ("C", 0, 1), ("Y", 0, 1), ("C", 0, 2), ("Y", 0, 2), ("Z", 1, 0), ("C", 1, 0),
    ("Y", 2, 0), ("Z", 3, 0), ("C", 2, 0), ("Y", 4, 0), ("Z", 5, 0), ("C", 3, 0), ("Y", 6, 0), ("Y", 7, 0),
    ("Z", 1, 1), ("C", 2, 1), ("Y", 4, 1), ("C", 1, 2), ("Z", 3, 2), ("C", 3, 1), ("Y", 7, 1), ("Z", 1, 2),
    ("C", 1, 1), ("Y", 2, 1), ("C", 3, 2), ("Y", 7, 2), ("Y", 2, 2), ("Z", 3, 1), ("Y", 6, 2), ("C", 1, 3),
    ("Y", 2, 3), ("Y", 6, 1), ("Z", 5, 1), ("Z", 0, 0), ("C", 3, 3), ("Y", 7, 3), ("Z", 2, 0), ("Z", 4, 0),
    ("Z", 7, 0), ("Z", 6, 0), ("Z", 0, 1), ("Z", 2, 1), ("Z", 3, 3), ("C", 0, 3), ("Z", 1, 3), ("C", 2, 2),
    ("Z", 5, 2), ("Y", 0, 3), ("Y", 4, 2), ("Z", 2, 2), ("Z", 7, 1), ("Z", 0, 2), ("Z", 4, 1), ("Z", 6, 1),
    ("F", 3, 0), ("C", 2, 3), ("Z", 5, 3), ("Y", 6, 3), ("Z", 7, 2), ("F", 1, 0), ("Z", 2, 3), ("F", 2, 0),
    ("Z", 0, 3), ("F", 0, 0), ("G", 3, 1), ("Z", 6, 2), ("Z", 4, 2), ("F", 5, 0), ("Z", 7, 3), ("F", 7, 0),
    ("Y", 4, 3), ("G", 1, 1), ("G", 2, 1), ("G", 0, 1), ("H", 3, 0), ("H", 5, 0), ("H", 7, 0), ("Z", 6, 3),
    ("H", 0, 0), ("H", 2, 0), ("F", 6, 0), ("Z", 4, 3), ("F", 4, 0), ("G", 1, 2), ("K", 5, 1), ("G", 7, 1),
    ("H", 2, 1), ("G", 0, 2), ("G", 5, 1), ("H", 0, 1), ("G", 6, 1), ("G", 3, 2), ("G", 4, 1), ("G", 2, 2),
    ("G", 4, 2), ("H", 6, 0), ("G", 1, 3), ("H", 1, 1), ("H", 4, 0), ("H", 1, 0), ("G", 0, 3), ("K", 7, 1),
    ("G", 6, 2), ("K", 3, 1), ("G", 5, 2), ("D", 0, 0), ("G", 2, 3), ("K", 3, 2), ("D", 2, 0), ("K", 7, 2),
    ("G", 4, 3), ("H", 0, 2), ("H", 6, 1), ("K", 5, 2), ("G", 7, 2), ("H", 4, 1), ("G", 6, 3), ("D", 3, 0),
    ("K", 3, 3), ("G", 3, 3), ("H", 2, 2), ("H", 1, 2), ("G", 5, 3), ("H", 1, 3), ("K", 5, 3), ("H", 0, 3),
    ("K", 7, 3), ("H", 4, 2), ("G", 7, 3), ("H", 6, 2), ("H", 2, 3), ("D", 1, 0), ("H", 4, 3), ("H", 6, 3),
    ("D", 4, 0),
)


def plan(Z):
    if 1 + max(s for _, _, s in TUNED) == Z:
        return BATCHES, TUNED
    units, parts = range(len(UNITS)), range(len(PARTS))
    order = [("C", u, None) for u in units]
    order += [("Y", q, None) for q in parts if PARTS[q][3] == "A"]
    for q in parts:
        order += [("Z", q, None), ("Z", q, Z - 1), ("F", q, 0)]
    for q in parts:
        order += [("G", q, None)]
        order += [("H", q, None)] if PARTS[q][4] == "A" else [("H", q, 0), ("K", q, None)]
    return ((0, len(UNITS), 0, Z),), order + [("D", 0, 0)]


def offsets(sizes):
    return [sum(sizes[:i]) for i in range(len(sizes) + 1)]


def kernel(
    Z,
    Y,
    replicas,
    tokens,
    pseudo_keys,
    pseudo_values,
    master_keys,
    moment_keys,
    master_values,
    moment_values,
    hyper_in,
    evals,
    states,
    tok,
    mine,
    from_core,
    to_y,
    from_y,
    to_z,
    from_left,
    from_right,
    weights,
    total,
    acc,
    master,
    moment,
    hyper,
    load_sem,
    state_sem,
    tok_sem,
    rc_s,
    rc_r,
    sends,
    ry_r,
    z_r,
    gy_r,
    gc_r,
):
    me = lax.axis_index("replica")
    core = lax.rem(me, 2)
    chip = lax.div(me, 2)
    y = lax.rem(chip, Y)
    z = lax.div(chip, Y)
    oc = 1 - core
    oy = 1 - y

    def dev(zz, yy, cc):
        return {"replica": (zz * Y + yy) * 2 + cc}

    pseudo = (pseudo_keys, pseudo_values)
    units = len(UNITS)
    rows, cols = mine.shape[3:]
    count = acc.shape[1]
    depth = 2 * rows
    batches, order = plan(Z)

    def lanes(u):
        return pl.ds(UNITS[u][1] * cols, cols)

    def edge(eighths):
        return rows if eighths == 8 else rows * eighths // 8 // 16 * 16

    spans = [pl.ds(edge(first), edge(last) - edge(first)) for _, first, last, _, _ in PARTS]
    unit = [part[0] for part in PARTS]
    reduce = [part[3] for part in PARTS]
    gather = [part[4] for part in PARTS]
    used = [q for q in range(len(PARTS)) if spans[q].size]

    loads = [
        pltpu.make_async_copy(
            pseudo[kv].at[:, :, core, :, lanes(u)], mine.at[u], load_sem.at[u]
        )
        for u, (kv, _) in enumerate(UNITS)
    ]
    state_loads = [
        pltpu.make_async_copy(src, dst, state_sem.at[i])
        for i, (src, dst) in enumerate(
            (
                (master_keys, master.at[0]),
                (moment_keys, moment.at[0]),
                (master_values, master.at[1]),
                (moment_values, moment.at[1]),
                (hyper_in, hyper),
            )
        )
    ]
    tok_load = pltpu.make_async_copy(tokens, tok, tok_sem)

    reduce_y_at = offsets([Z if kind == "A" else 1 for kind in reduce])
    gather_y_at = offsets([Z if kind == "A" else 1 for kind in gather])
    second_at = offsets([1 if kind == "A" else Z for kind in gather])

    upper = 2 * z >= Z
    m = jnp.minimum(z, Z - 1 - z)

    def near(s):
        half = (s + 1) // 2 if isinstance(s, int) else lax.div(s + 1, 2)
        side = 2 * (s % 2) - 1 if isinstance(s, int) else 2 * lax.rem(s, 2) - 1
        place = jnp.where(s <= 2 * m, m + half * side, s)
        return jnp.where(upper, Z - 1 - place, place)

    def far(s):
        return near(Z - 1 - s)

    def remote(src, dst, send, recv, device):
        return pltpu.make_async_remote_copy(
            src_ref=src,
            dst_ref=dst,
            send_sem=send,
            recv_sem=recv,
            device_id=device,
            device_id_type=MESH,
        )

    def core_copy(u, p):
        return remote(
            pseudo[UNITS[u][0]].at[p, :, oc, :, lanes(u)],
            from_core.at[u, p],
            rc_s,
            rc_r.at[u, p],
            dev(z, y, oc),
        )

    def y_copy(q, p):
        index = (unit[q], p, spans[q])
        slot = reduce_y_at[q] + (p if reduce[q] == "A" else 0)
        return remote(
            to_y.at[index], from_y.at[index], sends.at[q], ry_r.at[slot], dev(z, oy, core)
        )

    def second(q, p):
        return len(PARTS) * Z + second_at[q] + (p if gather[q] == "B" else 0)

    def z_refs(q, p):
        index = (unit[q], p, 0 if reduce[q] == "A" else slice(None), spans[q])
        return to_z.at[index], from_left.at[index], from_right.at[index]

    def right_copy(q, p):
        src, dst, _ = z_refs(q, p)
        return remote(src, dst, sends.at[q], z_r.at[q * Z + p], dev(z + 1, y, core))

    def left_copy(q, p, to):
        src, _, dst = z_refs(q, p)
        slot = jnp.where(p == to, second(q, p), q * Z + p)
        return remote(src, dst, sends.at[q], z_r.at[slot], dev(z - 1, y, core))

    def block(q, p, yy, cc):
        return weights.at[((unit[q] * Z + p) * Y + yy) * 2 + cc, spans[q]]

    def w_z(q, p, col, zz):
        w = block(q, p, oy if col else y, core)
        slot = second(q, p) if col else q * Z + p
        return remote(w, w, sends.at[q], z_r.at[slot], dev(zz, y, core))

    def w_y(q, p, yy):
        w = block(q, p, yy, core)
        slot = gather_y_at[q] + (p if gather[q] == "A" else 0)
        return remote(w, w, sends.at[q], gy_r.at[slot], dev(z, oy, core))

    def w_core(q, p, yy):
        w = block(q, p, yy, core)
        return remote(w, w, sends.at[q], gc_r.at[unit[q] * Z + p], dev(z, y, oc))

    def each(first, last, body):
        def run(s, carry):
            body(s)
            return carry

        lax.fori_loop(first, last, run, 0)

    for copy in loads:
        copy.start()

    @functools.partial(each, 0, units)
    def _(u):
        @functools.partial(each, 0, count // 128)
        def _(i):
            acc[u, pl.ds(pl.multiple_of(i * 128, 128), 128), :] = jnp.zeros((128, cols), F32)

    barrier = pltpu.get_barrier_semaphore()
    pl.semaphore_signal(barrier, inc=1, device_id=dev(z, y, oc), device_id_type=MESH)
    pl.semaphore_signal(barrier, inc=1, device_id=dev(z, oy, core), device_id_type=MESH)

    @pl.when(z > 0)
    def _():
        pl.semaphore_signal(barrier, inc=1, device_id=dev(z - 1, y, core), device_id_type=MESH)

    @pl.when(z < Z - 1)
    def _():
        pl.semaphore_signal(barrier, inc=1, device_id=dev(z + 1, y, core), device_id_type=MESH)

    peers = 2 + jnp.where(z > 0, 1, 0) + jnp.where(z < Z - 1, 1, 0)
    pl.semaphore_wait(barrier, peers)

    for u in range(units):
        each(0, Z, lambda s: core_copy(u, far(s)).start())
    for copy in state_loads + [tok_load]:
        copy.start()

    loaded = set()

    def once(name, copy):
        if name not in loaded:
            loaded.add(name)
            copy.wait()

    def pair_sum(q, p, yy):
        index = (unit[q], p, yy, spans[q])
        return mine[index].astype(F32) + from_core[index].astype(F32)

    def reduce_y(q, s):
        p = far(s)
        to_y[unit[q], p, spans[q]] = pair_sum(q, p, oy).astype(BF16)
        y_copy(q, p).start()

    def reduce_z(q, s, last):
        p = far(s)
        u = unit[q]
        first = reduce[q] == "A"
        if first:
            y_copy(q, p).wait_recv()
            part = total.at[u, y, spans[q]]
            part[...] = pair_sum(q, p, y) + from_y[u, p, spans[q]].astype(F32)
        else:
            part = total.at[u, :, spans[q]]
            part[...] = pair_sum(q, p, slice(None))
        out, left, right = z_refs(q, p)

        @pl.when((p >= z) & (z > 0))
        def _():
            right_copy(q, p).wait_recv()
            part[...] += left[...].astype(F32)

        @pl.when((p <= z) & (z < Z - 1))
        def _():
            left_copy(q, p, z).wait_recv()
            part[...] += right[...].astype(F32)

        if not last:
            out[...] = part[...].astype(BF16)

            @pl.when(p > z)
            def _():
                right_copy(q, p).start()

            @pl.when(p < z)
            def _():
                left_copy(q, p, z - 1).start()
        elif not first:
            to_y[u, z, spans[q]] = total[u, oy, spans[q]].astype(BF16)
            y_copy(q, z).start()

    def spread(q, p, col):
        @pl.when((p < z) & (z < Z - 1))
        def _():
            w_z(q, p, col, z + 1).start()

        @pl.when((p > z) & (z > 0))
        def _():
            w_z(q, p, col, z - 1).start()

    def spread_own(q, col):
        @pl.when(z < Z - 1)
        def _():
            w_z(q, z, col, z + 1).start()

        @pl.when(z > 0)
        def _():
            w_z(q, z, col, z - 1).start()

    def update(q):
        u, span = unit[q], spans[q]
        kv, lane = UNITS[u][0], lanes(u)
        summed = total[u, y, span]
        if reduce[q] == "B":
            y_copy(q, z).wait_recv()
            summed += from_y[u, z, span].astype(F32)
        for i in (4, 2 * kv, 2 * kv + 1):
            once(("state", i), state_loads[i])
        outer_rate = hyper[0]
        outer_mom = hyper[1]
        averaged = summed / replicas
        moment_new = outer_mom * moment[kv, span, lane] + averaged
        master_new = master[kv, span, lane] - outer_rate * (averaged + outer_mom * moment_new)
        block(q, z, y, core)[...] = master_new.astype(BF16)
        if gather[q] == "A":
            spread_own(q, 0)
            w_y(q, z, y).start()
        else:
            w_y(q, z, y).start()
            spread_own(q, 0)
        w_core(q, z, y).start()
        states[2 * kv, span, lane] = master_new
        states[2 * kv + 1, span, lane] = moment_new

    def pass_z(q, s, col):
        p = near(s)
        w_z(q, p, col, z).wait_recv()
        spread(q, p, col)
        if gather[q] == "A":
            w_y(q, p, y).start()
        w_core(q, p, oy if col else y).start()

    def pass_y(q, s):
        p = near(s)
        w_y(q, p, oy).wait_recv()
        if gather[q] == "B":
            spread_own(q, 1)
        w_core(q, p, oy).start()

    tile = min(1024, count)

    def products(u0, u1, s0, s1):
        def one(t):
            u = u0 + lax.rem(t, u1 - u0)
            p = near(s0 + lax.div(t, u1 - u0))
            w = weights.at[:Y]
            remote(w, w, rc_s, gc_r.at[u * Z + p], dev(z, y, oc)).wait_recv()
            kv = lax.div(u, units // 2)
            lane = pl.ds(pl.multiple_of(lax.rem(u, units // 2) * cols, cols), cols)

            def strip(i):
                at = pl.ds(i * tile if isinstance(i, int) else pl.multiple_of(i * tile, tile), tile)
                part = acc[u, at, :]
                for yy in range(Y):
                    place = p * Y + yy
                    if len(tok.shape) == 3:
                        left = tok[place, at, :]
                    else:
                        left = tok[at, pl.ds(pl.multiple_of(place * depth, depth), depth)]
                    right = weights[pl.ds(((u * Z + p) * Y + yy) * 2, 2)].reshape(depth, cols)
                    part += jnp.dot(left, right, preferred_element_type=F32)
                acc[u, at, :] = part
                evals[kv, at, lane] = part.astype(BF16)

            if count == tile:
                strip(0)
            else:
                each(0, count // tile, strip)

        each(0, (u1 - u0) * (s1 - s0), one)

    def drain():
        remote(from_core, from_core, rc_s, rc_s, dev(z, y, oc)).wait_send()

        def sent(q, blocks):
            w = weights.at[:blocks, spans[q]]
            remote(w, w, sends.at[q], sends.at[q], dev(z, y, oc)).wait_send()

        for inner in (True, False):

            @pl.when(((z > 0) & (z < Z - 1)) == inner)
            def _():
                for q in used:
                    beside = Z + 1 if inner else 1
                    across = beside + Z if gather[q] == "A" else 2 * beside + 1
                    sent(q, 2 * Z - 1 + across + 2 * Z)

    def take(kind, i, s):
        if kind == "C":
            once(i, loads[i])
            if s is None:
                each(0, Z, lambda t: core_copy(i, far(t)).wait_recv())
            else:
                core_copy(i, far(s)).wait_recv()
        elif kind == "Y":
            if s is None:
                each(0, Z, lambda t: reduce_y(i, t))
            else:
                reduce_y(i, s)
        elif kind == "Z":
            if s is None:
                each(0, Z - 1, lambda t: reduce_z(i, t, False))
            else:
                reduce_z(i, s, s == Z - 1)
        elif kind == "F":
            update(i)
        elif kind in ("G", "K"):
            col = 0 if kind == "G" else 1
            if s is None:
                each(1, Z, lambda t: pass_z(i, t, col))
            else:
                pass_z(i, s, col)
        elif kind == "H":
            if s is None:
                each(0, Z, lambda t: pass_y(i, t))
            else:
                pass_y(i, s)
        else:
            once("tokens", tok_load)
            products(*batches[i])

    for kind, i, s in order:
        if kind in "CD" or i in used:
            take(kind, i, s)
    drain()


def place(evals, states, *refs):
    target, sem = refs[:6], refs[6]
    source = [evals.at[i] for i in range(2)] + [states.at[i] for i in range(4)]
    stores = [pltpu.make_async_copy(source[i], target[i], sem.at[i]) for i in range(6)]
    for copy in stores:
        copy.start()
    for copy in stores:
        copy.wait()


def body(
    tokens,
    pseudo_keys,
    pseudo_values,
    master_keys,
    moment_keys,
    master_values,
    moment_values,
    outer_hyper,
):
    replicas = lax.axis_size("replica")
    Y = 2
    Z = replicas // (2 * Y)
    width = master_keys.shape[1]
    rows = master_keys.shape[0]
    count = tokens.shape[0]
    units = len(UNITS)
    parts = len(PARTS)
    cols = 2 * width // units
    depth = 2 * rows
    if depth % 128:
        tokens = tokens.reshape(count, Z * Y, depth).swapaxes(0, 1)
    pseudo_keys, pseudo_values = (
        p.reshape(Z, Y, 2, rows, width) for p in (pseudo_keys, pseudo_values)
    )
    hbm = pl.BlockSpec(memory_space=pltpu.HBM)
    vmem = pl.BlockSpec(memory_space=pltpu.VMEM)
    dma = pltpu.SemaphoreType.DMA
    state = (master_keys.shape, F32)
    evaluated = ((count, width), BF16)
    shapes = (evaluated, evaluated, state, state, state, state)
    single = pltpu.VMEM((units, Z, rows, cols), BF16)
    double = pltpu.VMEM((units, Z, Y, rows, cols), BF16)
    results = pl.pallas_call(
        functools.partial(kernel, Z, Y, replicas),
        out_shape=(pltpu.VMEM((2, count, width), BF16), pltpu.VMEM((4, rows, width), F32)),
        in_specs=[hbm] * 8,
        out_specs=(vmem,) * 2,
        scratch_shapes=[
            pltpu.VMEM(tokens.shape, BF16),
            double,
            double,
            single,
            single,
            double,
            double,
            double,
            pltpu.VMEM((units * Z * Y * 2, rows, cols), BF16),
            pltpu.VMEM((units, Y, rows, cols), F32),
            pltpu.VMEM((units, count, cols), F32),
            pltpu.VMEM((2, rows, width), F32),
            pltpu.VMEM((2, rows, width), F32),
            pltpu.SMEM((2,), F32),
            dma((units,)),
            dma((5,)),
            dma,
            dma,
            dma((units, Z)),
            dma((parts,)),
            dma((sum(Z if part[3] == "A" else 1 for part in PARTS),)),
            dma((parts * Z + sum(1 if part[4] == "A" else Z for part in PARTS),)),
            dma((sum(Z if part[4] == "A" else 1 for part in PARTS),)),
            dma((units * Z,)),
        ],
        compiler_params=pltpu.CompilerParams(
            collective_id=0, has_side_effects=True, vmem_limit_bytes=50 * 1024 * 1024
        ),
        name="outer_step",
    )(
        *[
            pltpu.with_memory_space_constraint(a, pltpu.HBM)
            for a in (
                tokens,
                pseudo_keys,
                pseudo_values,
                master_keys,
                moment_keys,
                master_values,
                moment_values,
                outer_hyper,
            )
        ]
    )
    return pl.pallas_call(
        place,
        out_shape=tuple(jax.ShapeDtypeStruct(*a) for a in shapes),
        in_specs=[vmem] * 2,
        out_specs=(hbm,) * 6,
        scratch_shapes=[dma((6,))],
        name="place",
    )(*[pltpu.with_memory_space_constraint(r, pltpu.VMEM) for r in results])


def solution(mesh):
    rows = P(("groups", "replica"), None)
    stack = P(("groups", "replica"), None, None)
    return jax.shard_map(
        body,
        mesh=mesh,
        in_specs=(rows, stack, stack, rows, rows, rows, rows, P("groups")),
        out_specs=(rows,) * 6,
        check_vma=False,
    )
```

time: 59.9 us -> 54 us (0.902)
  Pallas kernels: 59.2 us -> 53.2 us
    pallas_call x1, Pallas kernels: 57.5 us -> 51.5 us  [body(): pl.pallas_call(functools.partial(kernel, Z, Y, replicas), out_shape=(pltp...]
where the time goes in v2:
time: 54 us; the launch traced here: 53.9 us
  Pallas kernels  53.2 us (99%)
  between operations  0.64 us (1%)
    pallas_call x1, Pallas kernels, body(): pl.pallas_call(functools.partial(kernel, Z, Y, replicas), out_shape=(pltp...  51.5 us
    pallas_call x1, Pallas kernels, body(): pl.pallas_call(place, out_shape=tuple((jax.ShapeDtypeStruct(*a) for a in...  1.71 us

profile of v2, /device:TPU:0, one launch (start us, length us, event | category | flops | bytes accessed | tf_op | source)
XLA Modules:
  0.0 53.9 jit_solution(6522353232975675818)
XLA Ops:
  0.6 51.5 %outer_step.1 = (bf16[2,1024,512]{2,1,0:T(8,128)(2,1)S(1)}, f32[4,128,512]{2,1,0:T(8,128)S(1)}) custom-call(bf16[1024,2048]{1,0:T(8,128)(2,1)} %tokens.1, bf16[4,2,2,128,512]{4,3,2,1,0:T(8,128)(2,1)} %bitcast.2, bf16[4,2,2,128,512]{4,3,2,1,0:T(8,128)(2,1)} %bitcast.3, f32[128,512]{1,0:T(8,128)} %master_keys.1, f32[128,512]{1,0:T(8,128)} %moment_keys.1, ...), custom_call_target="tpu_custom_call" | custom-call | tf_op jit(solution)/shard_map/outer_step/pallas_call | solution.py:509
  52.2 1.7 %place.1 = (bf16[1024,512]{1,0:T(8,128)(2,1)}, bf16[1024,512]{1,0:T(8,128)(2,1)}, f32[128,512]{1,0:T(8,128)}, f32[128,512]{1,0:T(8,128)}, f32[128,512]{1,0:T(8,128)}, /*index=5*/f32[128,512]{1,0:T(8,128)}) custom-call(bf16[2,1024,512]{2,1,0:T(8,128)(2,1)S(1)} %get-tuple-element.8.evals, f32[4,128,512]{2,1,0:T(8,128)S(1)} %get-tuple-element.9.states), custom_call_target="tpu_custom_call" | custom-call | tf_op jit(solution)/shard_map/place/pallas_call | solution.py:559

commit v3 on v2

--- a/solution.py
+++ b/solution.py
@@ -23,26 +23,26 @@
     (3, 6, 8, "A", "B"),
 )
 
-BATCHES = ((0, 2, 0, 2), (0, 2, 2, 4), (2, 4, 0, 1), (2, 4, 1, 2), (2, 4, 2, 4))
+BATCHES = ((0, 2, 0, 1), (0, 2, 1, 2), (0, 2, 2, 3), (0, 2, 3, 4), (2, 4, 0, 1), (2, 4, 1, 2), (2, 4, 2, 3), (2, 4, 3, 4))
 TUNED = (
     ("C", 0, 0), ("Y", 0, 0), ("C", 0, 1), ("Y", 0, 1), ("C", 0, 2), ("Y", 0, 2), ("Z", 1, 0), ("C", 1, 0),
     ("Y", 2, 0), ("Z", 3, 0), ("C", 2, 0), ("Y", 4, 0), ("Z", 5, 0), ("C", 3, 0), ("Y", 6, 0), ("Y", 7, 0),
-    ("Z", 1, 1), ("C", 2, 1), ("Y", 4, 1), ("C", 1, 2), ("Z", 3, 2), ("C", 3, 1), ("Y", 7, 1), ("Z", 1, 2),
-    ("C", 1, 1), ("Y", 2, 1), ("C", 3, 2), ("Y", 7, 2), ("Y", 2, 2), ("Z", 3, 1), ("Y", 6, 2), ("C", 1, 3),
-    ("Y", 2, 3), ("Y", 6, 1), ("Z", 5, 1), ("Z", 0, 0), ("C", 3, 3), ("Y", 7, 3), ("Z", 2, 0), ("Z", 4, 0),
-    ("Z", 7, 0), ("Z", 6, 0), ("Z", 0, 1), ("Z", 2, 1), ("Z", 3, 3), ("C", 0, 3), ("Z", 1, 3), ("C", 2, 2),
-    ("Z", 5, 2), ("Y", 0, 3), ("Y", 4, 2), ("Z", 2, 2), ("Z", 7, 1), ("Z", 0, 2), ("Z", 4, 1), ("Z", 6, 1),
-    ("F", 3, 0), ("C", 2, 3), ("Z", 5, 3), ("Y", 6, 3), ("Z", 7, 2), ("F", 1, 0), ("Z", 2, 3), ("F", 2, 0),
-    ("Z", 0, 3), ("F", 0, 0), ("G", 3, 1), ("Z", 6, 2), ("Z", 4, 2), ("F", 5, 0), ("Z", 7, 3), ("F", 7, 0),
-    ("Y", 4, 3), ("G", 1, 1), ("G", 2, 1), ("G", 0, 1), ("H", 3, 0), ("H", 5, 0), ("H", 7, 0), ("Z", 6, 3),
-    ("H", 0, 0), ("H", 2, 0), ("F", 6, 0), ("Z", 4, 3), ("F", 4, 0), ("G", 1, 2), ("K", 5, 1), ("G", 7, 1),
-    ("H", 2, 1), ("G", 0, 2), ("G", 5, 1), ("H", 0, 1), ("G", 6, 1), ("G", 3, 2), ("G", 4, 1), ("G", 2, 2),
-    ("G", 4, 2), ("H", 6, 0), ("G", 1, 3), ("H", 1, 1), ("H", 4, 0), ("H", 1, 0), ("G", 0, 3), ("K", 7, 1),
-    ("G", 6, 2), ("K", 3, 1), ("G", 5, 2), ("D", 0, 0), ("G", 2, 3), ("K", 3, 2), ("D", 2, 0), ("K", 7, 2),
-    ("G", 4, 3), ("H", 0, 2), ("H", 6, 1), ("K", 5, 2), ("G", 7, 2), ("H", 4, 1), ("G", 6, 3), ("D", 3, 0),
-    ("K", 3, 3), ("G", 3, 3), ("H", 2, 2), ("H", 1, 2), ("G", 5, 3), ("H", 1, 3), ("K", 5, 3), ("H", 0, 3),
-    ("K", 7, 3), ("H", 4, 2), ("G", 7, 3), ("H", 6, 2), ("H", 2, 3), ("D", 1, 0), ("H", 4, 3), ("H", 6, 3),
-    ("D", 4, 0),
+    ("C", 1, 1), ("Y", 2, 1), ("Z", 3, 1), ("C", 2, 2), ("Y", 4, 2), ("C", 3, 1), ("Y", 7, 1), ("C", 1, 2),
+    ("Z", 3, 2), ("Z", 0, 0), ("Z", 1, 1), ("Z", 1, 2), ("C", 2, 1), ("Y", 4, 1), ("Z", 2, 0), ("C", 3, 2),
+    ("Y", 7, 2), ("Y", 2, 2), ("Z", 4, 0), ("Y", 6, 1), ("Z", 6, 0), ("Z", 7, 0), ("Z", 5, 1), ("C", 0, 3),
+    ("Y", 0, 3), ("Z", 0, 1), ("Z", 1, 3), ("Z", 2, 1), ("Z", 5, 2), ("C", 1, 3), ("Z", 3, 3), ("Z", 4, 1),
+    ("Z", 0, 2), ("Y", 2, 3), ("Y", 6, 2), ("Z", 2, 2), ("Z", 7, 1), ("C", 2, 3), ("Z", 5, 3), ("Z", 6, 1),
+    ("F", 1, 0), ("F", 3, 0), ("Z", 4, 2), ("Y", 4, 3), ("Z", 0, 3), ("F", 0, 0), ("C", 3, 3), ("Y", 6, 3),
+    ("G", 1, 1), ("Z", 2, 3), ("G", 3, 1), ("F", 5, 0), ("Z", 7, 2), ("Y", 7, 3), ("Z", 6, 2), ("H", 3, 0),
+    ("F", 2, 0), ("G", 0, 1), ("Z", 4, 3), ("F", 4, 0), ("G", 1, 2), ("G", 5, 1), ("H", 5, 0), ("Z", 7, 3),
+    ("F", 7, 0), ("Z", 6, 3), ("K", 3, 1), ("H", 1, 0), ("F", 6, 0), ("G", 0, 2), ("H", 2, 0), ("G", 2, 1),
+    ("G", 3, 2), ("G", 4, 1), ("G", 5, 2), ("H", 1, 1), ("K", 3, 2), ("G", 6, 1), ("H", 7, 0), ("G", 7, 1),
+    ("G", 2, 2), ("H", 0, 0), ("H", 6, 0), ("K", 5, 1), ("G", 4, 2), ("H", 4, 0), ("G", 6, 2), ("K", 5, 2),
+    ("G", 0, 3), ("G", 1, 3), ("G", 7, 2), ("H", 0, 2), ("D", 4, 0), ("K", 7, 1), ("H", 0, 1), ("H", 1, 2),
+    ("G", 2, 3), ("H", 2, 1), ("K", 7, 2), ("H", 4, 1), ("D", 0, 0), ("G", 4, 3), ("H", 6, 1), ("D", 1, 0),
+    ("G", 6, 3), ("H", 2, 2), ("D", 5, 0), ("K", 7, 3), ("H", 4, 2), ("G", 3, 3), ("D", 2, 0), ("H", 6, 2),
+    ("K", 3, 3), ("G", 5, 3), ("G", 7, 3), ("H", 0, 3), ("K", 5, 3), ("H", 2, 3), ("H", 1, 3), ("H", 4, 3),
+    ("D", 6, 0), ("H", 6, 3), ("D", 3, 0), ("D", 7, 0),
 )
 
 
@@ -118,7 +118,7 @@
     units = len(UNITS)
     rows, cols = mine.shape[3:]
     count = acc.shape[1]
-    depth = 2 * rows
+    depth = 2 * Y * rows
     batches, order = plan(Z)
 
     def lanes(u):
@@ -379,33 +379,29 @@
 
     def products(u0, u1, s0, s1):
         def one(t):
-            u = u0 + lax.rem(t, u1 - u0)
-            p = near(s0 + lax.div(t, u1 - u0))
-            w = weights.at[:Y]
-            remote(w, w, rc_s, gc_r.at[u * Z + p], dev(z, y, oc)).wait_recv()
-            kv = lax.div(u, units // 2)
-            lane = pl.ds(pl.multiple_of(lax.rem(u, units // 2) * cols, cols), cols)
+            p = near(s0 + t)
+            for u in range(u0, u1):
+                w = weights.at[:Y]
+                remote(w, w, rc_s, gc_r.at[u * Z + p], dev(z, y, oc)).wait_recv()
 
             def strip(i):
                 at = pl.ds(i * tile if isinstance(i, int) else pl.multiple_of(i * tile, tile), tile)
-                part = acc[u, at, :]
-                for yy in range(Y):
-                    place = p * Y + yy
-                    if len(tok.shape) == 3:
-                        left = tok[place, at, :]
-                    else:
-                        left = tok[at, pl.ds(pl.multiple_of(place * depth, depth), depth)]
-                    right = weights[pl.ds(((u * Z + p) * Y + yy) * 2, 2)].reshape(depth, cols)
-                    part += jnp.dot(left, right, preferred_element_type=F32)
-                acc[u, at, :] = part
-                evals[kv, at, lane] = part.astype(BF16)
+                if len(tok.shape) == 3:
+                    left = tok[p, at, :]
+                else:
+                    left = tok[at, pl.ds(pl.multiple_of(p * depth, depth), depth)]
+                for u in range(u0, u1):
+                    right = weights[pl.ds((u * Z + p) * 2 * Y, 2 * Y)].reshape(depth, cols)
+                    part = acc[u, at, :] + jnp.dot(left, right, preferred_element_type=F32)
+                    acc[u, at, :] = part
+                    evals[UNITS[u][0], at, lanes(u)] = part.astype(BF16)
 
             if count == tile:
                 strip(0)
             else:
                 each(0, count // tile, strip)
 
-        each(0, (u1 - u0) * (s1 - s0), one)
+        each(0, s1 - s0, one)
 
     def drain():
         remote(from_core, from_core, rc_s, rc_s, dev(z, y, oc)).wait_send()
@@ -492,9 +488,9 @@
     units = len(UNITS)
     parts = len(PARTS)
     cols = 2 * width // units
-    depth = 2 * rows
+    depth = 2 * Y * rows
     if depth % 128:
-        tokens = tokens.reshape(count, Z * Y, depth).swapaxes(0, 1)
+        tokens = tokens.reshape(count, Z, depth).swapaxes(0, 1)
     pseudo_keys, pseudo_values = (
         p.reshape(Z, Y, 2, rows, width) for p in (pseudo_keys, pseudo_values)
     )

time: 54 us -> 52.5 us (0.972)
  Pallas kernels: 53.2 us -> 51.7 us
    pallas_call x1, Pallas kernels: 51.5 us -> 50 us  [body(): pl.pallas_call(functools.partial(kernel, Z, Y, replicas), out_shape=(pltp...]
where the time goes in v3:
time: 52.5 us; the launch traced here: 52.3 us
  Pallas kernels  51.7 us (98%)
  between operations  0.64 us (1%)
    pallas_call x1, Pallas kernels, body(): pl.pallas_call(functools.partial(kernel, Z, Y, replicas), out_shape=(pltp...  50 us
    pallas_call x1, Pallas kernels, body(): pl.pallas_call(place, out_shape=tuple((jax.ShapeDtypeStruct(*a) for a in...  1.71 us

profile of v3, /device:TPU:0, one launch (start us, length us, event | category | flops | bytes accessed | tf_op | source)
XLA Modules:
  0.0 52.3 jit_solution(7886491235043134244)
XLA Ops:
  0.6 50.0 %outer_step.1 = (bf16[2,1024,512]{2,1,0:T(8,128)(2,1)S(1)}, f32[4,128,512]{2,1,0:T(8,128)S(1)}) custom-call(bf16[1024,2048]{1,0:T(8,128)(2,1)} %tokens.1, bf16[4,2,2,128,512]{4,3,2,1,0:T(8,128)(2,1)} %bitcast.2, bf16[4,2,2,128,512]{4,3,2,1,0:T(8,128)(2,1)} %bitcast.3, f32[128,512]{1,0:T(8,128)} %master_keys.1, f32[128,512]{1,0:T(8,128)} %moment_keys.1, ...), custom_call_target="tpu_custom_call" | custom-call | tf_op jit(solution)/shard_map/outer_step/pallas_call | solution.py:505
  50.6 1.7 %place.1 = (bf16[1024,512]{1,0:T(8,128)(2,1)}, bf16[1024,512]{1,0:T(8,128)(2,1)}, f32[128,512]{1,0:T(8,128)}, f32[128,512]{1,0:T(8,128)}, f32[128,512]{1,0:T(8,128)}, /*index=5*/f32[128,512]{1,0:T(8,128)}) custom-call(bf16[2,1024,512]{2,1,0:T(8,128)(2,1)S(1)} %get-tuple-element.8.evals, f32[4,128,512]{2,1,0:T(8,128)S(1)} %get-tuple-element.9.states), custom_call_target="tpu_custom_call" | custom-call | tf_op jit(solution)/shard_map/place/pallas_call | solution.py:555

commit v4 on v3

--- a/solution.py
+++ b/solution.py
@@ -23,26 +23,26 @@
     (3, 6, 8, "A", "B"),
 )
 
-BATCHES = ((0, 2, 0, 1), (0, 2, 1, 2), (0, 2, 2, 3), (0, 2, 3, 4), (2, 4, 0, 1), (2, 4, 1, 2), (2, 4, 2, 3), (2, 4, 3, 4))
+BATCHES = ((0, 0, 1), (0, 1, 2), (0, 2, 3), (0, 3, 4), (1, 0, 1), (1, 1, 2), (1, 2, 3), (1, 3, 4))
 TUNED = (
-    ("C", 0, 0), ("Y", 0, 0), ("C", 0, 1), ("Y", 0, 1), ("C", 0, 2), ("Y", 0, 2), ("Z", 1, 0), ("C", 1, 0),
-    ("Y", 2, 0), ("Z", 3, 0), ("C", 2, 0), ("Y", 4, 0), ("Z", 5, 0), ("C", 3, 0), ("Y", 6, 0), ("Y", 7, 0),
-    ("C", 1, 1), ("Y", 2, 1), ("Z", 3, 1), ("C", 2, 2), ("Y", 4, 2), ("C", 3, 1), ("Y", 7, 1), ("C", 1, 2),
-    ("Z", 3, 2), ("Z", 0, 0), ("Z", 1, 1), ("Z", 1, 2), ("C", 2, 1), ("Y", 4, 1), ("Z", 2, 0), ("C", 3, 2),
-    ("Y", 7, 2), ("Y", 2, 2), ("Z", 4, 0), ("Y", 6, 1), ("Z", 6, 0), ("Z", 7, 0), ("Z", 5, 1), ("C", 0, 3),
-    ("Y", 0, 3), ("Z", 0, 1), ("Z", 1, 3), ("Z", 2, 1), ("Z", 5, 2), ("C", 1, 3), ("Z", 3, 3), ("Z", 4, 1),
-    ("Z", 0, 2), ("Y", 2, 3), ("Y", 6, 2), ("Z", 2, 2), ("Z", 7, 1), ("C", 2, 3), ("Z", 5, 3), ("Z", 6, 1),
-    ("F", 1, 0), ("F", 3, 0), ("Z", 4, 2), ("Y", 4, 3), ("Z", 0, 3), ("F", 0, 0), ("C", 3, 3), ("Y", 6, 3),
-    ("G", 1, 1), ("Z", 2, 3), ("G", 3, 1), ("F", 5, 0), ("Z", 7, 2), ("Y", 7, 3), ("Z", 6, 2), ("H", 3, 0),
-    ("F", 2, 0), ("G", 0, 1), ("Z", 4, 3), ("F", 4, 0), ("G", 1, 2), ("G", 5, 1), ("H", 5, 0), ("Z", 7, 3),
-    ("F", 7, 0), ("Z", 6, 3), ("K", 3, 1), ("H", 1, 0), ("F", 6, 0), ("G", 0, 2), ("H", 2, 0), ("G", 2, 1),
-    ("G", 3, 2), ("G", 4, 1), ("G", 5, 2), ("H", 1, 1), ("K", 3, 2), ("G", 6, 1), ("H", 7, 0), ("G", 7, 1),
-    ("G", 2, 2), ("H", 0, 0), ("H", 6, 0), ("K", 5, 1), ("G", 4, 2), ("H", 4, 0), ("G", 6, 2), ("K", 5, 2),
-    ("G", 0, 3), ("G", 1, 3), ("G", 7, 2), ("H", 0, 2), ("D", 4, 0), ("K", 7, 1), ("H", 0, 1), ("H", 1, 2),
-    ("G", 2, 3), ("H", 2, 1), ("K", 7, 2), ("H", 4, 1), ("D", 0, 0), ("G", 4, 3), ("H", 6, 1), ("D", 1, 0),
-    ("G", 6, 3), ("H", 2, 2), ("D", 5, 0), ("K", 7, 3), ("H", 4, 2), ("G", 3, 3), ("D", 2, 0), ("H", 6, 2),
-    ("K", 3, 3), ("G", 5, 3), ("G", 7, 3), ("H", 0, 3), ("K", 5, 3), ("H", 2, 3), ("H", 1, 3), ("H", 4, 3),
-    ("D", 6, 0), ("H", 6, 3), ("D", 3, 0), ("D", 7, 0),
+    ("C", 0, 0), ("Y", 0, 0), ("C", 0, 3), ("Y", 0, 3), ("C", 1, 0), ("Y", 2, 0), ("C", 0, 1), ("Y", 0, 1),
+    ("Z", 3, 0), ("C", 2, 0), ("Y", 4, 0), ("Z", 1, 0), ("C", 3, 0), ("Y", 6, 0), ("Z", 5, 0), ("C", 1, 2),
+    ("Y", 2, 2), ("Y", 7, 0), ("C", 1, 1), ("Z", 3, 1), ("C", 3, 1), ("Y", 7, 1), ("C", 0, 2), ("Y", 0, 2),
+    ("Y", 2, 1), ("C", 2, 1), ("Y", 4, 1), ("Z", 0, 0), ("Z", 1, 1), ("Z", 3, 2), ("Z", 1, 2), ("Z", 2, 0),
+    ("C", 3, 3), ("Y", 6, 3), ("Z", 4, 0), ("Y", 6, 1), ("Z", 6, 0), ("Z", 5, 1), ("C", 1, 3), ("Z", 3, 3),
+    ("C", 2, 2), ("Y", 4, 2), ("Z", 7, 0), ("Y", 2, 3), ("Z", 0, 1), ("Z", 5, 2), ("Z", 2, 1), ("Z", 1, 3),
+    ("C", 3, 2), ("Y", 6, 2), ("Z", 4, 1), ("Z", 0, 2), ("Z", 6, 1), ("Z", 2, 2), ("Z", 7, 1), ("F", 3, 0),
+    ("C", 2, 3), ("Z", 5, 3), ("Y", 7, 2), ("Y", 4, 3), ("Z", 4, 2), ("F", 1, 0), ("Z", 0, 3), ("F", 0, 0),
+    ("Z", 6, 2), ("H", 3, 0), ("Y", 7, 3), ("F", 5, 0), ("Z", 2, 3), ("G", 3, 1), ("Z", 7, 2), ("F", 2, 0),
+    ("G", 1, 1), ("Z", 4, 3), ("F", 4, 0), ("G", 0, 1), ("G", 1, 2), ("H", 5, 0), ("Z", 6, 3), ("F", 6, 0),
+    ("H", 0, 0), ("Z", 7, 3), ("F", 7, 0), ("G", 2, 1), ("G", 0, 2), ("G", 4, 1), ("G", 2, 2), ("H", 1, 0),
+    ("G", 5, 1), ("H", 0, 1), ("K", 5, 1), ("H", 6, 0), ("H", 2, 0), ("G", 6, 1), ("G", 4, 2), ("H", 7, 0),
+    ("G", 6, 2), ("K", 5, 2), ("G", 5, 2), ("H", 1, 1), ("H", 1, 2), ("G", 1, 3), ("G", 0, 3), ("H", 4, 0),
+    ("D", 0, 0), ("G", 3, 2), ("G", 2, 3), ("D", 4, 0), ("H", 2, 1), ("K", 3, 2), ("H", 0, 2), ("K", 3, 1),
+    ("G", 4, 3), ("D", 1, 0), ("G", 6, 3), ("H", 4, 1), ("K", 7, 1), ("H", 2, 2), ("G", 7, 1), ("G", 7, 2),
+    ("K", 7, 2), ("H", 6, 1), ("D", 2, 0), ("K", 3, 3), ("H", 4, 2), ("G", 5, 3), ("H", 6, 2), ("K", 5, 3),
+    ("D", 5, 0), ("H", 1, 3), ("G", 3, 3), ("G", 7, 3), ("H", 0, 3), ("K", 7, 3), ("H", 2, 3), ("H", 4, 3),
+    ("D", 6, 0), ("H", 6, 3), ("D", 3, 0),
 )
 
 
@@ -57,11 +57,30 @@
     for q in parts:
         order += [("G", q, None)]
         order += [("H", q, None)] if PARTS[q][4] == "A" else [("H", q, 0), ("K", q, None)]
-    return ((0, len(UNITS), 0, Z),), order + [("D", 0, 0)]
+    return ((0, 0, Z), (1, 0, Z - 1)), order + [("D", 0, 0), ("D", 1, 0)]
 
 
 def offsets(sizes):
     return [sum(sizes[:i]) for i in range(len(sizes) + 1)]
+
+
+def partial_product(tok, held, h, p, Z, at):
+    blocks = 2 * 2
+    depth = blocks * held.shape[1]
+    if len(tok.shape) == 3:
+        left = tok[p, at, :]
+    else:
+        left = tok[at, pl.ds(pl.multiple_of(p * depth, depth), depth)]
+    right = held[pl.ds((h * Z + p) * blocks, blocks)].reshape(depth, held.shape[2])
+    return jnp.dot(left, right, preferred_element_type=F32)
+
+
+def near_step(z, s, Z):
+    m = jnp.minimum(z, Z - 1 - z)
+    half = (s + 1) // 2 if isinstance(s, int) else lax.div(s + 1, 2)
+    side = 2 * (s % 2) - 1 if isinstance(s, int) else 2 * lax.rem(s, 2) - 1
+    place = jnp.where(s <= 2 * m, m + half * side, s)
+    return jnp.where(2 * z >= Z, Z - 1 - place, place)
 
 
 def kernel(
@@ -79,6 +98,8 @@
     evals,
     states,
     tok,
+    values,
+    totals,
     mine,
     from_core,
     to_y,
@@ -118,7 +139,6 @@
     units = len(UNITS)
     rows, cols = mine.shape[3:]
     count = acc.shape[1]
-    depth = 2 * Y * rows
     batches, order = plan(Z)
 
     def lanes(u):
@@ -157,14 +177,8 @@
     gather_y_at = offsets([Z if kind == "A" else 1 for kind in gather])
     second_at = offsets([1 if kind == "A" else Z for kind in gather])
 
-    upper = 2 * z >= Z
-    m = jnp.minimum(z, Z - 1 - z)
-
     def near(s):
-        half = (s + 1) // 2 if isinstance(s, int) else lax.div(s + 1, 2)
-        side = 2 * (s % 2) - 1 if isinstance(s, int) else 2 * lax.rem(s, 2) - 1
-        place = jnp.where(s <= 2 * m, m + half * side, s)
-        return jnp.where(upper, Z - 1 - place, place)
+        return near_step(z, s, Z)
 
     def far(s):
         return near(Z - 1 - s)
@@ -212,7 +226,9 @@
         return remote(src, dst, sends.at[q], z_r.at[slot], dev(z - 1, y, core))
 
     def block(q, p, yy, cc):
-        return weights.at[((unit[q] * Z + p) * Y + yy) * 2 + cc, spans[q]]
+        kv, h = UNITS[unit[q]]
+        held = values if kv else weights
+        return held.at[((h * Z + p) * Y + yy) * 2 + cc, spans[q]]
 
     def w_z(q, p, col, zz):
         w = block(q, p, oy if col else y, core)
@@ -226,7 +242,7 @@
 
     def w_core(q, p, yy):
         w = block(q, p, yy, core)
-        return remote(w, w, sends.at[q], gc_r.at[unit[q] * Z + p], dev(z, y, oc))
+        return remote(w, w, sends.at[q], gc_r.at[UNITS[unit[q]][0] * Z + p], dev(z, y, oc))
 
     def each(first, last, body):
         def run(s, carry):
@@ -238,11 +254,12 @@
     for copy in loads:
         copy.start()
 
-    @functools.partial(each, 0, units)
-    def _(u):
-        @functools.partial(each, 0, count // 128)
-        def _(i):
-            acc[u, pl.ds(pl.multiple_of(i * 128, 128), 128), :] = jnp.zeros((128, cols), F32)
+    @functools.partial(each, 0, count // 128)
+    def _(i):
+        at = pl.ds(pl.multiple_of(i * 128, 128), 128)
+        for h in range(units // 2):
+            acc[h, at, :] = jnp.zeros((128, cols), F32)
+            totals[h, at, :] = jnp.zeros((128, cols), F32)
 
     barrier = pltpu.get_barrier_semaphore()
     pl.semaphore_signal(barrier, inc=1, device_id=dev(z, y, oc), device_id_type=MESH)
@@ -377,24 +394,24 @@
 
     tile = min(1024, count)
 
-    def products(u0, u1, s0, s1):
+    def arrived(kv, p):
+        w = weights.at[: units // 2 * Y] if kv == 0 else values.at[: units // 2 * Y]
+        remote(w, w, rc_s, gc_r.at[kv * Z + p], dev(z, y, oc)).wait_recv()
+
+    def products(kv, s0, s1):
         def one(t):
             p = near(s0 + t)
-            for u in range(u0, u1):
-                w = weights.at[:Y]
-                remote(w, w, rc_s, gc_r.at[u * Z + p], dev(z, y, oc)).wait_recv()
+            arrived(kv, p)
 
             def strip(i):
                 at = pl.ds(i * tile if isinstance(i, int) else pl.multiple_of(i * tile, tile), tile)
-                if len(tok.shape) == 3:
-                    left = tok[p, at, :]
-                else:
-                    left = tok[at, pl.ds(pl.multiple_of(p * depth, depth), depth)]
-                for u in range(u0, u1):
-                    right = weights[pl.ds((u * Z + p) * 2 * Y, 2 * Y)].reshape(depth, cols)
-                    part = acc[u, at, :] + jnp.dot(left, right, preferred_element_type=F32)
-                    acc[u, at, :] = part
-                    evals[UNITS[u][0], at, lanes(u)] = part.astype(BF16)
+                for h in range(units // 2):
+                    part = product(h, p, at, kv)
+                    if kv:
+                        totals[h, at, :] = part
+                    else:
+                        acc[h, at, :] = part
+                        evals[at, h * cols : (h + 1) * cols] = part.astype(BF16)
 
             if count == tile:
                 strip(0)
@@ -402,6 +419,10 @@
                 each(0, count // tile, strip)
 
         each(0, s1 - s0, one)
+
+    def product(h, p, at, kv):
+        sums, held = (totals, values) if kv else (acc, weights)
+        return sums[h, at, :] + partial_product(tok, held, h, p, Z, at)
 
     def drain():
         remote(from_core, from_core, rc_s, rc_s, dev(z, y, oc)).wait_send()
@@ -456,15 +477,29 @@
     for kind, i, s in order:
         if kind in "CD" or i in used:
             take(kind, i, s)
+    arrived(1, near(Z - 1))
     drain()
 
 
-def place(evals, states, *refs):
-    target, sem = refs[:6], refs[6]
-    source = [evals.at[i] for i in range(2)] + [states.at[i] for i in range(4)]
-    stores = [pltpu.make_async_copy(source[i], target[i], sem.at[i]) for i in range(6)]
+def place(Z, Y, evals, states, tok, values, totals, *refs):
+    target, result, sem = refs[:6], refs[6], refs[7]
+    tile = min(512, result.shape[0])
+    cols = values.shape[2]
+    stores = [pltpu.make_async_copy(evals, target[0], sem.at[0])]
+    stores += [
+        pltpu.make_async_copy(states.at[i], target[2 + i], sem.at[1 + i]) for i in range(4)
+    ]
     for copy in stores:
         copy.start()
+    p = near_step(lax.div(lax.axis_index("replica"), 2 * Y), Z - 1, Z)
+    for i in range(result.shape[0] // tile):
+        at = pl.ds(i * tile, tile)
+        for h in range(totals.shape[0]):
+            part = totals[h, at, :] + partial_product(tok, values, h, p, Z, at)
+            result[at, h * cols : (h + 1) * cols] = part.astype(BF16)
+        copy = pltpu.make_async_copy(result.at[at], target[1].at[at], sem.at[5 + i])
+        copy.start()
+        stores.append(copy)
     for copy in stores:
         copy.wait()
 
@@ -486,6 +521,7 @@
     rows = master_keys.shape[0]
     count = tokens.shape[0]
     units = len(UNITS)
+    halves = units // 2
     parts = len(PARTS)
     cols = 2 * width // units
     depth = 2 * Y * rows
@@ -504,11 +540,16 @@
     double = pltpu.VMEM((units, Z, Y, rows, cols), BF16)
     results = pl.pallas_call(
         functools.partial(kernel, Z, Y, replicas),
-        out_shape=(pltpu.VMEM((2, count, width), BF16), pltpu.VMEM((4, rows, width), F32)),
+        out_shape=(
+            pltpu.VMEM((count, width), BF16),
+            pltpu.VMEM((4, rows, width), F32),
+            pltpu.VMEM(tokens.shape, BF16),
+            pltpu.VMEM((halves * Z * Y * 2, rows, cols), BF16),
+            pltpu.VMEM((halves, count, cols), F32),
+        ),
         in_specs=[hbm] * 8,
-        out_specs=(vmem,) * 2,
+        out_specs=(vmem,) * 5,
         scratch_shapes=[
-            pltpu.VMEM(tokens.shape, BF16),
             double,
             double,
             single,
@@ -516,9 +557,9 @@
             double,
             double,
             double,
-            pltpu.VMEM((units * Z * Y * 2, rows, cols), BF16),
+            pltpu.VMEM((halves * Z * Y * 2, rows, cols), BF16),
             pltpu.VMEM((units, Y, rows, cols), F32),
-            pltpu.VMEM((units, count, cols), F32),
+            pltpu.VMEM((halves, count, cols), F32),
             pltpu.VMEM((2, rows, width), F32),
             pltpu.VMEM((2, rows, width), F32),
             pltpu.SMEM((2,), F32),
@@ -531,10 +572,10 @@
             dma((sum(Z if part[3] == "A" else 1 for part in PARTS),)),
             dma((parts * Z + sum(1 if part[4] == "A" else Z for part in PARTS),)),
             dma((sum(Z if part[4] == "A" else 1 for part in PARTS),)),
-            dma((units * Z,)),
+            dma((2 * Z,)),
         ],
         compiler_params=pltpu.CompilerParams(
-            collective_id=0, has_side_effects=True, vmem_limit_bytes=50 * 1024 * 1024
+            collective_id=0, has_side_effects=True, vmem_limit_bytes=30 * 1024 * 1024
         ),
         name="outer_step",
     )(
@@ -553,11 +594,15 @@
         ]
     )
     return pl.pallas_call(
-        place,
+        functools.partial(place, Z, Y),
         out_shape=tuple(jax.ShapeDtypeStruct(*a) for a in shapes),
-        in_specs=[vmem] * 2,
+        in_specs=[vmem] * 5,
         out_specs=(hbm,) * 6,
-        scratch_shapes=[dma((6,))],
+        scratch_shapes=[
+            pltpu.VMEM((count, width), BF16),
+            dma((5 + count // min(512, count),)),
+        ],
+        compiler_params=pltpu.CompilerParams(vmem_limit_bytes=14 * 1024 * 1024),
         name="place",
     )(*[pltpu.with_memory_space_constraint(r, pltpu.VMEM) for r in results])
 

time: 52.5 us -> 51.7 us (0.985)
  Pallas kernels: 51.7 us -> 50.9 us
    pallas_call x1, Pallas kernels: 50 us -> 49.2 us  [body(): pl.pallas_call(functools.partial(kernel, Z, Y, replicas), out_shape=(pltp...]
where the time goes in v4:
time: 51.7 us; the launch traced here: 51.6 us
  Pallas kernels  50.9 us (98%)
  between operations  0.64 us (1%)
    pallas_call x1, Pallas kernels, body(): pl.pallas_call(functools.partial(kernel, Z, Y, replicas), out_shape=(pltp...  49.2 us
    pallas_call x1, Pallas kernels, body(): pl.pallas_call(functools.partial(place, Z, Y), out_shape=tuple((jax.Shape...  1.73 us

profile of v4, /device:TPU:0, one launch (start us, length us, event | category | flops | bytes accessed | tf_op | source)
XLA Modules:
  0.0 51.6 jit_solution(14198793934446542169)
XLA Ops:
  0.6 49.2 %outer_step.1 = (bf16[1024,512]{1,0:T(8,128)(2,1)S(1)}, f32[4,128,512]{2,1,0:T(8,128)S(1)}, bf16[1024,2048]{1,0:T(8,128)(2,1)S(1)}, bf16[32,128,256]{2,1,0:T(8,128)(2,1)S(1)}, f32[2,1024,256]{2,1,0:T(8,128)S(1)}) custom-call(bf16[1024,2048]{1,0:T(8,128)(2,1)} %tokens.1, bf16[4,2,2,128,512]{4,3,2,1,0:T(8,128)(2,1)} %bitcast.2, ...), custom_call_target="tpu_custom_call" | custom-call | tf_op jit(solution)/shard_map/outer_step/pallas_call | solution.py:541
  49.9 1.7 %place.1 = (bf16[1024,512]{1,0:T(8,128)(2,1)}, bf16[1024,512]{1,0:T(8,128)(2,1)}, f32[128,512]{1,0:T(8,128)}, f32[128,512]{1,0:T(8,128)}, f32[128,512]{1,0:T(8,128)}, /*index=5*/f32[128,512]{1,0:T(8,128)}) custom-call(bf16[1024,512]{1,0:T(8,128)(2,1)S(1)} %get-tuple-element.11.evals, f32[4,128,512]{2,1,0:T(8,128)S(1)} %get-tuple-element.12.states, ...), custom_call_target="tpu_custom_call" | custom-call | tf_op jit(solution)/shard_map/place/pallas_call | solution.py:596

commit v5 on v4

--- a/solution.py
+++ b/solution.py
@@ -13,36 +13,48 @@
 
 UNITS = ((0, 0), (0, 1), (1, 0), (1, 1))
 PARTS = (
-    (0, 0, 6, "A", "A"),
+    (0, 0, 3, "A", "A"),
+    (0, 3, 6, "A", "A"),
     (0, 6, 8, "B", "A"),
-    (1, 0, 6, "A", "A"),
+    (1, 0, 4, "A", "A"),
+    (1, 4, 6, "A", "A"),
     (1, 6, 8, "B", "B"),
-    (2, 0, 6, "A", "A"),
+    (2, 0, 4, "A", "A"),
+    (2, 4, 6, "A", "A"),
     (2, 6, 8, "B", "B"),
-    (3, 0, 6, "A", "A"),
-    (3, 6, 8, "A", "B"),
+    (3, 0, 3, "A", "A"),
+    (3, 3, 6, "A", "A"),
+    (3, 6, 8, "B", "B"),
 )
 
 BATCHES = ((0, 0, 1), (0, 1, 2), (0, 2, 3), (0, 3, 4), (1, 0, 1), (1, 1, 2), (1, 2, 3), (1, 3, 4))
 TUNED = (
-    ("C", 0, 0), ("Y", 0, 0), ("C", 0, 3), ("Y", 0, 3), ("C", 1, 0), ("Y", 2, 0), ("C", 0, 1), ("Y", 0, 1),
-    ("Z", 3, 0), ("C", 2, 0), ("Y", 4, 0), ("Z", 1, 0), ("C", 3, 0), ("Y", 6, 0), ("Z", 5, 0), ("C", 1, 2),
-    ("Y", 2, 2), ("Y", 7, 0), ("C", 1, 1), ("Z", 3, 1), ("C", 3, 1), ("Y", 7, 1), ("C", 0, 2), ("Y", 0, 2),
-    ("Y", 2, 1), ("C", 2, 1), ("Y", 4, 1), ("Z", 0, 0), ("Z", 1, 1), ("Z", 3, 2), ("Z", 1, 2), ("Z", 2, 0),
-    ("C", 3, 3), ("Y", 6, 3), ("Z", 4, 0), ("Y", 6, 1), ("Z", 6, 0), ("Z", 5, 1), ("C", 1, 3), ("Z", 3, 3),
-    ("C", 2, 2), ("Y", 4, 2), ("Z", 7, 0), ("Y", 2, 3), ("Z", 0, 1), ("Z", 5, 2), ("Z", 2, 1), ("Z", 1, 3),
-    ("C", 3, 2), ("Y", 6, 2), ("Z", 4, 1), ("Z", 0, 2), ("Z", 6, 1), ("Z", 2, 2), ("Z", 7, 1), ("F", 3, 0),
-    ("C", 2, 3), ("Z", 5, 3), ("Y", 7, 2), ("Y", 4, 3), ("Z", 4, 2), ("F", 1, 0), ("Z", 0, 3), ("F", 0, 0),
-    ("Z", 6, 2), ("H", 3, 0), ("Y", 7, 3), ("F", 5, 0), ("Z", 2, 3), ("G", 3, 1), ("Z", 7, 2), ("F", 2, 0),
-    ("G", 1, 1), ("Z", 4, 3), ("F", 4, 0), ("G", 0, 1), ("G", 1, 2), ("H", 5, 0), ("Z", 6, 3), ("F", 6, 0),
-    ("H", 0, 0), ("Z", 7, 3), ("F", 7, 0), ("G", 2, 1), ("G", 0, 2), ("G", 4, 1), ("G", 2, 2), ("H", 1, 0),
-    ("G", 5, 1), ("H", 0, 1), ("K", 5, 1), ("H", 6, 0), ("H", 2, 0), ("G", 6, 1), ("G", 4, 2), ("H", 7, 0),
-    ("G", 6, 2), ("K", 5, 2), ("G", 5, 2), ("H", 1, 1), ("H", 1, 2), ("G", 1, 3), ("G", 0, 3), ("H", 4, 0),
-    ("D", 0, 0), ("G", 3, 2), ("G", 2, 3), ("D", 4, 0), ("H", 2, 1), ("K", 3, 2), ("H", 0, 2), ("K", 3, 1),
-    ("G", 4, 3), ("D", 1, 0), ("G", 6, 3), ("H", 4, 1), ("K", 7, 1), ("H", 2, 2), ("G", 7, 1), ("G", 7, 2),
-    ("K", 7, 2), ("H", 6, 1), ("D", 2, 0), ("K", 3, 3), ("H", 4, 2), ("G", 5, 3), ("H", 6, 2), ("K", 5, 3),
-    ("D", 5, 0), ("H", 1, 3), ("G", 3, 3), ("G", 7, 3), ("H", 0, 3), ("K", 7, 3), ("H", 2, 3), ("H", 4, 3),
-    ("D", 6, 0), ("H", 6, 3), ("D", 3, 0),
+    ("C", 0, 0), ("Y", 1, 0), ("Y", 0, 0), ("C", 0, 1), ("Y", 1, 1), ("Y", 0, 1), ("C", 0, 2), ("Y", 0, 2),
+    ("Y", 1, 2), ("Z", 2, 0), ("C", 1, 0), ("Y", 4, 0), ("Y", 3, 0), ("Z", 5, 0), ("C", 2, 0), ("Y", 7, 0),
+    ("Y", 6, 0), ("Z", 8, 0), ("C", 3, 0), ("Y", 10, 0), ("Y", 9, 0), ("C", 2, 1), ("Y", 6, 1), ("Z", 11, 0),
+    ("Z", 2, 1), ("C", 2, 2), ("Y", 7, 2), ("Y", 7, 1), ("C", 0, 3), ("Y", 1, 3), ("C", 1, 3), ("Y", 4, 3),
+    ("C", 1, 1), ("Y", 4, 1), ("C", 3, 1), ("Y", 9, 1), ("Z", 0, 0), ("Z", 5, 1), ("C", 1, 2), ("Z", 5, 2),
+    ("C", 3, 2), ("Y", 9, 2), ("C", 2, 3), ("Y", 7, 3), ("Z", 1, 0), ("Y", 3, 1), ("Z", 4, 0), ("Y", 10, 1),
+    ("Y", 4, 2), ("Z", 3, 0), ("Y", 3, 3), ("Z", 7, 0), ("Z", 6, 0), ("Z", 10, 0), ("Z", 9, 0), ("Z", 1, 1),
+    ("Z", 0, 1), ("Y", 3, 2), ("Z", 8, 1), ("Z", 5, 3), ("Y", 0, 3), ("Z", 2, 2), ("Z", 4, 1), ("Y", 6, 3),
+    ("Y", 10, 2), ("Z", 11, 1), ("Z", 0, 2), ("Z", 7, 1), ("Z", 1, 2), ("Z", 3, 1), ("Z", 8, 2), ("Z", 4, 2),
+    ("Z", 11, 2), ("C", 3, 3), ("Y", 10, 3), ("Z", 2, 3), ("Z", 6, 1), ("Y", 6, 2), ("Z", 7, 2), ("Z", 9, 1),
+    ("F", 5, 0), ("Z", 1, 3), ("F", 1, 0), ("Z", 10, 1), ("Z", 0, 3), ("Z", 3, 2), ("Z", 8, 3), ("F", 0, 0),
+    ("Z", 4, 3), ("F", 4, 0), ("F", 2, 0), ("Z", 11, 3), ("G", 5, 1), ("Z", 6, 2), ("G", 1, 1), ("Z", 7, 3),
+    ("H", 5, 0), ("F", 7, 0), ("Y", 9, 3), ("Z", 9, 2), ("F", 8, 0), ("G", 4, 1), ("G", 0, 1), ("Z", 10, 2),
+    ("G", 2, 1), ("F", 11, 0), ("Z", 3, 3), ("F", 3, 0), ("K", 5, 1), ("G", 7, 1), ("H", 1, 0), ("G", 1, 2),
+    ("H", 8, 0), ("G", 8, 1), ("Z", 6, 3), ("F", 6, 0), ("G", 4, 2), ("G", 0, 2), ("G", 11, 1), ("H", 4, 1),
+    ("G", 3, 1), ("Z", 9, 3), ("F", 9, 0), ("H", 2, 0), ("Z", 10, 3), ("F", 10, 0), ("H", 2, 1), ("H", 1, 1),
+    ("G", 2, 2), ("G", 7, 2), ("G", 6, 1), ("H", 11, 0), ("K", 8, 1), ("G", 3, 2), ("H", 0, 2), ("H", 7, 0),
+    ("G", 9, 1), ("H", 4, 2), ("G", 6, 2), ("H", 0, 0), ("G", 10, 1), ("G", 9, 2), ("H", 4, 0), ("H", 0, 1),
+    ("G", 10, 2), ("G", 1, 3), ("G", 5, 2), ("H", 3, 1), ("H", 9, 0), ("H", 3, 0), ("G", 2, 3), ("K", 8, 2),
+    ("H", 6, 0), ("G", 0, 3), ("G", 4, 3), ("H", 10, 0), ("D", 0, 0), ("G", 3, 3), ("H", 2, 2), ("H", 7, 1),
+    ("G", 11, 2), ("G", 8, 2), ("K", 5, 2), ("H", 1, 2), ("G", 7, 3), ("D", 4, 0), ("G", 6, 3), ("H", 7, 2),
+    ("H", 3, 2), ("G", 9, 3), ("D", 1, 0), ("G", 10, 3), ("H", 6, 1), ("K", 11, 2), ("H", 9, 1),
+    ("K", 11, 1), ("H", 6, 2), ("H", 10, 1), ("D", 2, 0), ("G", 5, 3), ("G", 8, 3), ("H", 9, 2),
+    ("H", 10, 2), ("K", 8, 3), ("D", 5, 0), ("K", 5, 3), ("H", 2, 3), ("H", 1, 3), ("G", 11, 3), ("H", 0, 3),
+    ("K", 11, 3), ("H", 4, 3), ("H", 6, 3), ("H", 7, 3), ("H", 3, 3), ("D", 6, 0), ("H", 9, 3), ("H", 10, 3),
+    ("D", 3, 0),
 )
 
 

time: 51.7 us -> 51.2 us (level)
    pallas_call x1, Pallas kernels: 49.2 us -> 48.7 us  [body(): pl.pallas_call(functools.partial(kernel, Z, Y, replicas), out_shape=(pltp...]
where the time goes in v5:
time: 51.2 us; the launch traced here: 51 us
  Pallas kernels  50.4 us (98%)
  between operations  0.64 us (1%)
    pallas_call x1, Pallas kernels, body(): pl.pallas_call(functools.partial(kernel, Z, Y, replicas), out_shape=(pltp...  48.7 us
    pallas_call x1, Pallas kernels, body(): pl.pallas_call(functools.partial(place, Z, Y), out_shape=tuple((jax.Shape...  1.73 us

profile of v5, /device:TPU:0, one launch (start us, length us, event | category | flops | bytes accessed | tf_op | source)
XLA Modules:
  0.0 51.0 jit_solution(17360696338479553555)
XLA Ops:
  0.6 48.7 %outer_step.1 = (bf16[1024,512]{1,0:T(8,128)(2,1)S(1)}, f32[4,128,512]{2,1,0:T(8,128)S(1)}, bf16[1024,2048]{1,0:T(8,128)(2,1)S(1)}, bf16[32,128,256]{2,1,0:T(8,128)(2,1)S(1)}, f32[2,1024,256]{2,1,0:T(8,128)S(1)}) custom-call(bf16[1024,2048]{1,0:T(8,128)(2,1)} %tokens.1, bf16[4,2,2,128,512]{4,3,2,1,0:T(8,128)(2,1)} %bitcast.2, ...), custom_call_target="tpu_custom_call" | custom-call | tf_op jit(solution)/shard_map/outer_step/pallas_call | solution.py:553
  49.3 1.7 %place.1 = (bf16[1024,512]{1,0:T(8,128)(2,1)}, bf16[1024,512]{1,0:T(8,128)(2,1)}, f32[128,512]{1,0:T(8,128)}, f32[128,512]{1,0:T(8,128)}, f32[128,512]{1,0:T(8,128)}, /*index=5*/f32[128,512]{1,0:T(8,128)}) custom-call(bf16[1024,512]{1,0:T(8,128)(2,1)S(1)} %get-tuple-element.11.evals, f32[4,128,512]{2,1,0:T(8,128)S(1)} %get-tuple-element.12.states, ...), custom_call_target="tpu_custom_call" | custom-call | tf_op jit(solution)/shard_map/place/pallas_call | solution.py:608
